TPU v7x, 8 devices: a whole 2x2x1 slice. The times are simulated.
8 devices in a mesh: dp: 1 (over z), tp: 2 (over y), sp: 4 (over x, core).
Axes of the slice: x: 2, y: 2, z: 1, core: 2. Of those that a mesh axis runs over, the one named last changes fastest.
Arguments:
- hidden: bfloat16 [128, 8192], P('dp')
- lengths: int32 [128], P('dp')
- k_cache: bfloat16 [128, 1024, 8, 128], P('dp', 'sp', 'tp')
- v_cache: bfloat16 [128, 1024, 8, 128], P('dp', 'sp', 'tp')
- norm_gain: bfloat16 [8192], replicated
- w_q: bfloat16 [8192, 8192], P(None, 'tp')
- w_k: bfloat16 [8192, 1024], P(None, 'tp')
- w_v: bfloat16 [8192, 1024], P(None, 'tp')
- w_o: bfloat16 [8192, 8192], P('tp')
- inv_freq: float32 [64], replicated
Outputs:
- output 1: bfloat16 [128, 8192], P('dp')
- output 2: bfloat16 [128, 1024, 8, 128], P('dp', 'sp', 'tp')
- output 3: bfloat16 [128, 1024, 8, 128], P('dp', 'sp', 'tp')
All inputs are finite; a program needn't handle non-finite values.
Results may differ from a plain program's by a relative error of at most 0.0085197.
Values sent between devices are 32-bit elements.
A program may use at most 1.25 GiB of HBM per device.

v0:
```python
import jax
import jax.numpy as jnp
from jax import lax
from jax.sharding import PartitionSpec as P

NORM_EPS = 1e-5
NEG_BIG = -1e30


def rms_norm(hidden, norm_gain):
    hidden_f32 = hidden.astype(jnp.float32)
    inv_rms = lax.rsqrt(jnp.mean(hidden_f32 * hidden_f32, axis=-1, keepdims=True) + NORM_EPS)
    return (hidden_f32 * inv_rms * norm_gain.astype(jnp.float32)).astype(jnp.bfloat16)


def apply_rope(head_vec, angles):
    half_dim = head_vec.shape[-1] // 2
    vec_f32 = head_vec.astype(jnp.float32)
    cos_ang = jnp.cos(angles)[:, None, :]
    sin_ang = jnp.sin(angles)[:, None, :]
    lo_half = vec_f32[..., :half_dim]
    hi_half = vec_f32[..., half_dim:]
    rotated = jnp.concatenate([lo_half * cos_ang - hi_half * sin_ang, hi_half * cos_ang + lo_half * sin_ang], axis=-1)
    return rotated.astype(jnp.bfloat16)


def project_new_token(hidden, lengths, norm_gain, w_q, w_k, w_v, inv_freq):
    batch_size = hidden.shape[0]
    head_dim = 2 * inv_freq.shape[0]
    normed = rms_norm(hidden, norm_gain)
    q_heads = jnp.dot(normed, w_q, preferred_element_type=jnp.float32).astype(jnp.bfloat16).reshape(batch_size, -1, head_dim)
    k_new = jnp.dot(normed, w_k, preferred_element_type=jnp.float32).astype(jnp.bfloat16).reshape(batch_size, -1, head_dim)
    v_new = jnp.dot(normed, w_v, preferred_element_type=jnp.float32).astype(jnp.bfloat16).reshape(batch_size, -1, head_dim)
    angles = lengths.astype(jnp.float32)[:, None] * inv_freq[None, :]
    return apply_rope(q_heads, angles), apply_rope(k_new, angles), v_new


def write_and_attend(q_rot, k_rot, v_new, lengths, k_cache, v_cache):
    batch_size, slot_count, kv_local, head_dim = k_cache.shape
    slot_start = lax.axis_index('sp') * slot_count
    local_pos = lengths - slot_start
    owned = (local_pos >= 0) & (local_pos < slot_count)
    write_pos = jnp.where(owned, local_pos, slot_count)
    row_ids = jnp.arange(batch_size)
    k_upd = k_cache.at[row_ids, write_pos].set(k_rot, mode='drop')
    v_upd = v_cache.at[row_ids, write_pos].set(v_new, mode='drop')
    group_size = q_rot.shape[1] // kv_local
    q_grp = q_rot.reshape(batch_size, kv_local, group_size, head_dim)
    scores = jnp.einsum('bkgd,bskd->bkgs', q_grp, k_upd, preferred_element_type=jnp.float32) * head_dim ** -0.5
    valid_mask = ((slot_start + jnp.arange(slot_count))[None, :] <= lengths[:, None])[:, None, None, :]
    scores = jnp.where(valid_mask, scores, NEG_BIG)
    part_max = jnp.max(scores, axis=-1)
    weights = jnp.where(valid_mask, jnp.exp(scores - part_max[..., None]), 0.0)
    part_sum = jnp.sum(weights, axis=-1)
    part_out = jnp.einsum('bkgs,bskd->bkgd', weights.astype(jnp.bfloat16), v_upd, preferred_element_type=jnp.float32)
    return k_upd, v_upd, part_max, part_sum, part_out


def device_step(hidden, lengths, k_cache, v_cache, norm_gain, w_q, w_k, w_v, w_o, inv_freq):
    batch_size = hidden.shape[0]
    q_rot, k_rot, v_new = project_new_token(hidden, lengths, norm_gain, w_q, w_k, w_v, inv_freq)
    k_upd, v_upd, part_max, part_sum, part_out = write_and_attend(q_rot, k_rot, v_new, lengths, k_cache, v_cache)
    all_max = lax.all_gather(part_max, 'sp')
    all_sum = lax.all_gather(part_sum, 'sp')
    all_out = lax.all_gather(part_out, 'sp')
    top_score = jnp.max(all_max, axis=0)
    factor = jnp.exp(all_max - top_score[None])
    weighted = jnp.sum(factor[..., None] * all_out, axis=0)
    weight_sum = jnp.sum(factor * all_sum, axis=0)
    attn_out = (weighted / weight_sum[..., None]).astype(jnp.bfloat16).reshape(batch_size, -1)
    proj_out = lax.psum(jnp.dot(attn_out, w_o, preferred_element_type=jnp.float32), 'tp')
    y_out = (hidden.astype(jnp.float32) + proj_out).astype(jnp.bfloat16)
    return y_out, k_upd, v_upd


def solution(mesh):
    cache_spec = P('dp', 'sp', 'tp', None)
    in_specs = (P('dp', None), P('dp'), cache_spec, cache_spec, P(None), P(None, 'tp'), P(None, 'tp'), P(None, 'tp'), P('tp', None), P(None))
    out_specs = (P('dp', None), cache_spec, cache_spec)
    return jax.shard_map(device_step, mesh=mesh, in_specs=in_specs, out_specs=out_specs, check_vma=False)
```

profile of v0, /device:TPU:0, one launch (start us, length us, event | category | flops | bytes accessed | tf_op | source)
XLA Modules:
  0.0 364.1 jit_solution(9842695475123791467)
XLA Ops:
  7.2 23.3 %copy.43 = bf16[128,256,4,128]{3,2,1,0:T(4,128)(2,1)} copy(bf16[128,256,4,128]{3,2,1,0:T(4,128)(2,1)} %param.13) | data formatting | bytes 67108864
  30.5 23.4 %copy.42 = bf16[128,256,4,128]{3,2,1,0:T(4,128)(2,1)} copy(bf16[128,256,4,128]{3,2,1,0:T(4,128)(2,1)} %param.12) | data formatting | bytes 67108864
  54.1 0.5 fusion.5
  54.6 4.8 %convolution_convert_fusion.1 = bf16[128,512]{1,0:T(8,128)(2,1)S(1)} fusion(bf16[8192,512]{1,0:T(8,128)(2,1)} %param.17, bf16[128,8192]{1,0:T(8,128)(2,1)S(1)} %copy-done, f32[8192]{0:T(1024)S(1)} %convert_element_type.51, f32[128]{0:T(128)S(1)} %add_rsqrt_fusion), kind=kOutput, calls=%fused_computation.30 | convolution fusion | flops 1078001664 | bytes 10650112 | tf_op jit(solution)/shard_map/dot_general | solution.py:33
  59.5 4.8 %fusion.19 = f32[128,512]{1,0:T(8,128)S(1)} fusion(bf16[8192,512]{1,0:T(8,128)(2,1)} %param.16, bf16[128,8192]{1,0:T(8,128)(2,1)S(1)} %copy-done, f32[8192]{0:T(1024)S(1)} %convert_element_type.51, f32[128]{0:T(128)S(1)} %add_rsqrt_fusion), kind=kOutput, calls=%fused_computation.32 | convolution fusion | flops 1078067200 | bytes 10781184 | tf_op jit(solution)/shard_map/dot_general | solution.py:32
  64.4 24.2 %fusion.18 = f32[16,8,32,128]{3,1,2,0:T(8,128)} fusion(bf16[8192,4096]{1,0:T(8,128)(2,1)} %param.15, bf16[128,8192]{1,0:T(8,128)(2,1)S(1)} %copy-done, f32[8192]{0:T(1024)S(1)} %convert_element_type.51, f32[128]{0:T(128)S(1)} %add_rsqrt_fusion), kind=kOutput, calls=%fused_computation.29 | convolution fusion | flops 8595177472 | bytes 71336448 | tf_op jit(solution)/shard_map/dot_general | solution.py:31
  88.6 2.0 copy.25
  90.5 0.3 multiply_cosine_fusion
  90.9 0.3 subtract_convert_fusion.1
  91.2 1.8 fusion.20
  93.1 15.8 %scatter_fusion.1 = bf16[128,256,4,128]{3,2,1,0:T(4,128)(2,1)} fusion(bf16[128,256,4,128]{3,2,1,0:T(4,128)(2,1)} %copy.43, s32[128]{0:T(128)S(1)} %fusion.32, bf16[128,4,128]{2,1,0:T(4,128)(2,1)S(1)} %reshape.119), kind=kCustom, calls=%fused_computation.1 | custom fusion | bytes 394240 | tf_op jit(solution)/shard_map/scatter | solution.py:46
  108.9 15.8 %scatter_fusion = bf16[128,256,4,128]{3,2,1,0:T(4,128)(2,1)} fusion(bf16[128,256,4,128]{3,2,1,0:T(4,128)(2,1)} %copy.42, s32[128]{0:T(128)S(1)} %fusion.32, bf16[128,4,128]{2,1,0:T(4,128)(2,1)S(1)} %pad_maximum_fusion), kind=kCustom, calls=%fused_computation | custom fusion | bytes 394240 | tf_op jit(solution)/shard_map/scatter | solution.py:45
  124.7 17.8 %fusion.9 = (f32[128,4,8]{2,1,0:T(4,128)S(1)}, f32[128,4,8,256]{3,2,1,0:T(8,128)}) fusion(pred[128,256]{1,0:T(8,128)(4,1)S(1)} %broadcast_compare_fusion, bf16[128,256,4,128]{3,2,1,0:T(4,128)(2,1)} %scatter_fusion, bf16[128,4,8,64]{3,2,1,0:T(8,128)(2,1)} %get-tuple-element.6, bf16[128,4,8,64]{3,2,1,0:T(8,128)(2,1)S(1)} %get-tuple-element.5), kind=kOutput, calls=%fused_computation.18 | convolution fusion | flops 273674240 | bytes 38846464 | tf_op jit(solution)/shard_map/bkgd,bskd->bkgs/dot_general | solution.py:49
  142.5 17.3 %fusion = f32[128,4,8,128]{3,2,1,0:T(8,128)} fusion(bf16[128,256,4,128]{3,2,1,0:T(4,128)(2,1)} %scatter_fusion.1, f32[128,4,8,256]{3,2,1,0:T(8,128)} %get-tuple-element.12, f32[128,4,8]{2,1,0:T(4,128)S(1)} %get-tuple-element.11, pred[128,256]{1,0:T(8,128)(4,1)S(1)} %broadcast_compare_fusion), kind=kOutput, calls=%fused_computation.2 | convolution fusion | flops 273678336 | bytes 39895040 | tf_op jit(solution)/shard_map/bkgs,bskd->bkgd/dot_general | solution.py:55
  159.9 3.4 fusion.10
  163.5 10.1 %all-gather.2 = f32[512,4,8]{0,2,1:T(8,128)S(1)} all-gather(f32[128,4,8]{0,2,1:T(8,128)S(1)} %copy.23), channel_id=4, replica_groups=mesh['dp'=1,'tp'=2,'sp'=4] {'sp'}, dimensions={0}, use_global_device_ids=true | all-gather | bytes 81920 | tf_op jit(solution)/shard_map/all_gather | solution.py:64
  173.6 8.0 %all-gather = f32[512,4,8]{0,2,1:T(8,128)S(1)} all-gather(f32[128,4,8]{0,2,1:T(8,128)S(1)} %copy.20), channel_id=2, replica_groups=mesh['dp'=1,'tp'=2,'sp'=4] {'sp'}, dimensions={0}, use_global_device_ids=true | all-gather | bytes 81920 | tf_op jit(solution)/shard_map/all_gather | solution.py:63
  181.7 0.4 copy.21
  182.2 37.4 %all-gather.5.cloned.1.call-done = f32[512,4,8,128]{3,2,1,0:T(8,128)} async-done(((f32[128,4,8,128]{3,2,1,0:T(8,128)}), f32[512,4,8,128]{3,2,1,0:T(8,128)}) %all-gather.5.cloned.1.call-update) | async-done | bytes 8388624 | tf_op jit(solution)/shard_map/all_gather | solution.py:65
  219.6 5.6 %multiply_reduce_fusion = f32[128,4,8,128]{3,2,1,0:T(8,128)S(1)} fusion(f32[4,128,4,8,128]{4,3,2,1,0:T(8,128)} %bitcast.34, f32[4,128,4,8]{3,2,1,0:T(4,128)S(1)} %copy.21), kind=kLoop, calls=%fused_computation.6 | loop fusion | flops 3670016 | bytes 10551296 | tf_op jit(solution)/shard_map/reduce_sum | solution.py:68
  225.3 0.7 divide_convert_fusion
  226.0 25.0 %fusion.22 = f32[128,8192]{1,0:T(8,128)} fusion(bf16[4096,8192]{1,0:T(8,128)(2,1)} %param.18, bf16[16,8,32,128]{3,2,1,0:T(8,128)(2,1)S(1)} %bitcast.35), kind=kOutput, calls=%fused_computation.35 | convolution fusion | flops 8589934592 | bytes 72351744 | tf_op jit(solution)/shard_map/dot_general | solution.py:71
  251.0 102.2 %all-reduce.2.cloned.1.call-done = f32[128,8192]{1,0:T(8,128)} async-done(((f32[128,8192]{1,0:T(8,128)}), f32[128,8192]{1,0:T(8,128)}) %all-reduce.2.cloned.1.call-update) | async-done | bytes 4194320 | tf_op jit(solution)/shard_map/psum | solution.py:71
  353.2 4.0 %fusion.8 = bf16[128,8192]{1,0:T(8,128)(2,1)} fusion(f32[128,8192]{1,0:T(8,128)} %all-reduce.2.cloned.1.call-done, bf16[128,8192]{1,0:T(8,128)(2,1)S(1)} %copy-done), kind=kLoop, calls=%fused_computation.15 | loop fusion | flops 3145728 | bytes 8388608 | tf_op jit(solution)/shard_map/convert_element_type | solution.py:72
  (26 shorter events, 0.9 us)
Async XLA Ops:
  7.2 212.4 %all-gather.5.cloned.1.call-start = ((), (), s32[]{:S(2)}) async-start(), calls=%async_computation.1 | async-start | bytes 10485760 | tf_op jit(solution)/shard_map/all_gather | solution.py:65
  30.5 23.5 %copy-start.2 = (s32[128]{0:T(128)S(1)}, s32[128]{0:T(128)}, u32[]{:S(2)}) copy-start(s32[128]{0:T(128)} %param.11) | copy-start | bytes 1540
  30.5 23.5 %copy-start.1 = (bf16[8192]{0:T(1024)(128)(2,1)S(1)}, bf16[8192]{0:T(1024)(128)(2,1)}, u32[]{:S(2)}) copy-start(bf16[8192]{0:T(1024)(128)(2,1)} %param.14) | copy-start | bytes 49156
  30.5 23.5 %copy-start = (bf16[128,8192]{1,0:T(8,128)(2,1)S(1)}, bf16[128,8192]{1,0:T(8,128)(2,1)}, u32[]{:S(2)}) copy-start(bf16[128,8192]{1,0:T(8,128)(2,1)} %param.10) | copy-start | bytes 6291460
  88.6 2.0 copy-start.3
  159.8 193.4 %all-reduce.2.cloned.1.call-start = ((), (), s32[]{:S(2)}) async-start(), calls=%async_computation | async-start | bytes 8388608 | tf_op jit(solution)/shard_map/psum | solution.py:71
Sparse Core Ops, SparseCore 0:
  159.9 59.6 all-gather.4
  251.1 102.0 all-reduce.1
where the time goes:
time: 365 us; the launch traced here: 364 us
  waiting for transfers between devices  140 us (38%)
  matrix products  93.9 us (26%)
  local copies, waits for them, and re-layouts  81.1 us (22%)
  blocking collectives  18.2 us (5%)
  other arithmetic  17 us (5%)
  between operations  14.2 us (4%)
    psum x1, waiting for transfers between devices, device_step(): lax.psum(jnp.dot(attn_out, w_o, preferred_element_type=jnp.float32), 'tp')  102 us
    unnamed x11, local copies, waits for them, and re-layouts  48.7 us
    all_gather x1, waiting for transfers between devices, device_step(): all_out = lax.all_gather(part_out, 'sp')  37.4 us
    dot_general x1, matrix products, device_step(): jnp.dot(attn_out, w_o, preferred_element_type=jnp.float32)  25 us
    dot_general x1, matrix products, project_new_token(): jnp.dot(normed, w_q, preferred_element_type=jnp.float32)  24.2 us
    dot_general x1, matrix products, write_and_attend(): jnp.einsum('bkgd,bskd->bkgs', q_grp, k_upd, preferred_element_type=jnp.fl...  17.8 us
    dot_general x1, matrix products, write_and_attend(): jnp.einsum('bkgs,bskd->bkgd', weights.astype(jnp.bfloat16), v_upd, prefer...  17.3 us
    scatter x1, local copies, waits for them, and re-layouts, write_and_attend(): v_upd = v_cache.at[row_ids, write_pos].set(v_new, mode='drop')  15.8 us
  transfers between devices with their start and end apart: 2, of which 2 were waited for; matrix products, arithmetic and copies ran while one was open for 1% of the time, Pallas kernels for 0%

commit v1 on v0

v1 whole, which is shorter than its diff:
```python
import functools

import jax
import jax.numpy as jnp
from jax import lax
from jax.experimental import pallas as pl
from jax.experimental.pallas import tpu as pltpu
from jax.sharding import PartitionSpec as P

NORM_EPS = 1e-5
NEG_BIG = -3.0e38
LOG2E = 1.4426950408889634
ANY = pl.BlockSpec(memory_space=pl.ANY)
VMEM = pl.BlockSpec(memory_space=pltpu.VMEM)
SMEM = pl.BlockSpec(memory_space=pltpu.SMEM)


def rms_norm(hidden, norm_gain):
    hidden_f32 = hidden.astype(jnp.float32)
    inv_rms = lax.rsqrt(jnp.mean(hidden_f32 * hidden_f32, axis=-1, keepdims=True) + NORM_EPS)
    return (hidden_f32 * inv_rms * norm_gain.astype(jnp.float32)).astype(jnp.bfloat16)


def apply_rope(head_vec, angles):
    half_dim = head_vec.shape[-1] // 2
    vec_f32 = head_vec.astype(jnp.float32)
    cos_ang = jnp.cos(angles)[:, None, :]
    sin_ang = jnp.sin(angles)[:, None, :]
    lo_half = vec_f32[..., :half_dim]
    hi_half = vec_f32[..., half_dim:]
    rotated = jnp.concatenate([lo_half * cos_ang - hi_half * sin_ang, hi_half * cos_ang + lo_half * sin_ang], axis=-1)
    return rotated.astype(jnp.bfloat16)


CHUNK = 8
NBUF = 6
LAG = 3


def attend_kernel(len_ref, q_ref, kv_ref, k_hbm, v_hbm, ko_hbm, vo_hbm, o_ref, st_ref,
                  kbuf, vbuf, obuf, mbuf, lbuf, in_sem, out_sem):
    batch, rows, head_dim = k_hbm.shape
    kv_local = kv_ref.shape[0] * kv_ref.shape[2] // 2
    heads = q_ref.shape[0] * q_ref.shape[2]
    slots = rows // kv_local
    steps = batch // CHUNK
    slot_start = lax.axis_index('sp') * slots

    def copies_in(i):
        b = lax.rem(i, NBUF)
        src = pl.ds(i * CHUNK, CHUNK)
        return (pltpu.make_async_copy(k_hbm.at[src], kbuf.at[b], in_sem.at[0, b]),
                pltpu.make_async_copy(v_hbm.at[src], vbuf.at[b], in_sem.at[1, b]))

    def copies_out(i):
        b = lax.rem(i, NBUF)
        dst = pl.ds(i * CHUNK, CHUNK)
        return (pltpu.make_async_copy(kbuf.at[b], ko_hbm.at[dst], out_sem.at[0, b]),
                pltpu.make_async_copy(vbuf.at[b], vo_hbm.at[dst], out_sem.at[1, b]))

    for i in range(NBUF - LAG):
        for c in copies_in(i):
            c.start()

    col = lax.broadcasted_iota(jnp.int32, (heads, rows), 1)
    row = lax.broadcasted_iota(jnp.int32, (heads, rows), 0)
    head_ok = lax.rem(col, kv_local) == row // (heads // kv_local)
    tile_slot = lax.broadcasted_iota(jnp.int32, (16, head_dim), 0) // kv_local
    lane = lax.broadcasted_iota(jnp.int32, (heads, batch), 1)
    score_scale = head_dim ** -0.5 * LOG2E

    def step(i, carry):
        buf = lax.rem(i, NBUF)

        @pl.when((i >= LAG) & (i + NBUF - LAG < steps))
        def _():
            for c in copies_out(i - LAG):
                c.wait()

        @pl.when(i + NBUF - LAG < steps)
        def _():
            for c in copies_in(i + NBUF - LAG):
                c.start()

        for c in copies_in(i):
            c.wait()
        for s in range(CHUNK):
            b = i * CHUNK + s
            pos = len_ref[b] - slot_start
            own = (pos >= 0) & (pos < slots)
            safe = jnp.where(own, pos, 0)
            per_tile = 16 // kv_local
            base = pl.multiple_of(safe // per_tile * 16, 16)
            pick = (tile_slot == lax.rem(safe, per_tile)) & own
            new0 = kv_ref[0, b]
            new1 = kv_ref[1, b]
            for dst, lo in ((kbuf, 0), (vbuf, kv_local // 2)):
                new = jnp.concatenate([new0[lo:lo + kv_local // 2], new1[lo:lo + kv_local // 2]] * per_tile, axis=0)
                old = dst[buf, s, pl.ds(base, 16), :].astype(jnp.float32)
                dst[buf, s, pl.ds(base, 16), :] = jnp.where(pick, new, old).astype(jnp.bfloat16)
        m_all, l_all = mbuf[...], lbuf[...]
        for s in range(0, CHUNK, 2):
            b0 = i * CHUNK + s
            b1 = b0 + 1
            limit0 = (len_ref[b0] - slot_start + 1) * kv_local
            limit1 = (len_ref[b1] - slot_start + 1) * kv_local
            q0 = jnp.concatenate([q_ref[0, b0], q_ref[1, b0]], axis=0).astype(jnp.bfloat16)
            q1 = jnp.concatenate([q_ref[0, b1], q_ref[1, b1]], axis=0).astype(jnp.bfloat16)
            zero = jnp.zeros_like(q0)
            q = jnp.concatenate([jnp.concatenate([q0, zero], axis=1), jnp.concatenate([zero, q1], axis=1)], axis=0)
            k = jnp.concatenate([kbuf[buf, s], kbuf[buf, s + 1]], axis=1)
            v = jnp.concatenate([vbuf[buf, s], vbuf[buf, s + 1]], axis=1)
            scores = lax.dot_general(q, k, (((1,), (1,)), ((), ())), preferred_element_type=jnp.float32)
            valid = jnp.concatenate([head_ok & (col < limit0), head_ok & (col < limit1)], axis=0)
            scores = jnp.where(valid, scores * score_scale, NEG_BIG)
            top = jnp.max(scores, axis=-1, keepdims=True)
            weights = jnp.where(valid, jnp.exp2(scores - top), 0.0)
            total = jnp.sum(weights, axis=-1, keepdims=True)
            out = jnp.dot(weights.astype(jnp.bfloat16), v, preferred_element_type=jnp.float32)
            obuf[s] = out[:heads, :head_dim]
            obuf[s + 1] = out[heads:, head_dim:]
            m_all = jnp.where(lane == b0, top[:heads], jnp.where(lane == b1, top[heads:], m_all))
            l_all = jnp.where(lane == b0, total[:heads], jnp.where(lane == b1, total[heads:], l_all))
        mbuf[...] = m_all
        lbuf[...] = l_all
        o_ref[:, pl.ds(pl.multiple_of(i * CHUNK, CHUNK), CHUNK), :] = jnp.swapaxes(obuf[...], 0, 1)
        for c in copies_out(i):
            c.start()

        return carry

    mbuf[...] = jnp.zeros_like(mbuf)
    lbuf[...] = jnp.zeros_like(lbuf)
    lax.fori_loop(0, steps, step, 0)
    for i in range(steps - NBUF, steps):
        for c in copies_out(i):
            c.wait()
    st_ref[0] = mbuf[...].T
    st_ref[1] = lbuf[...].T


def write_and_attend(lengths, q_all, kv_all, k_cache, v_cache):
    batch, slots, kv_local, head_dim = k_cache.shape
    heads = q_all.shape[0] * q_all.shape[2]
    rows = slots * kv_local
    flat = (batch, rows, head_dim)
    out_shape = (jax.ShapeDtypeStruct(flat, k_cache.dtype), jax.ShapeDtypeStruct(flat, v_cache.dtype),
                 jax.ShapeDtypeStruct((heads, batch, head_dim), jnp.float32),
                 jax.ShapeDtypeStruct((2, batch, heads), jnp.float32))
    k_new, v_new, o, stats = pl.pallas_call(
        attend_kernel,
        out_shape=out_shape,
        in_specs=[SMEM, VMEM, VMEM, ANY, ANY],
        out_specs=(ANY, ANY, VMEM, VMEM),
        scratch_shapes=[
            pltpu.VMEM((NBUF, CHUNK, rows, head_dim), jnp.bfloat16),
            pltpu.VMEM((NBUF, CHUNK, rows, head_dim), jnp.bfloat16),
            pltpu.VMEM((CHUNK, heads, head_dim), jnp.float32),
            pltpu.VMEM((heads, batch), jnp.float32),
            pltpu.VMEM((heads, batch), jnp.float32),
            pltpu.SemaphoreType.DMA((2, NBUF)),
            pltpu.SemaphoreType.DMA((2, NBUF)),
        ],
        compiler_params=pltpu.CompilerParams(vmem_limit_bytes=56 * 1024 * 1024),
        cost_estimate=pl.CostEstimate(flops=4 * batch * heads * rows * head_dim, bytes_accessed=8 * batch * rows * head_dim, transcendentals=0),
        name='attend',
    )(lengths, q_all, kv_all, k_cache.reshape(flat), v_cache.reshape(flat))
    return k_new.reshape(k_cache.shape), v_new.reshape(v_cache.shape), o, stats


PIECES = 4
MESH = pl.DeviceIdType.MESH


def combine_kernel(o_ref, st_ref, w_hbm, hid_hbm, y_ref, w, hid, r1, st1, c1, stc, r2, st2, att, lhs, part, r3, yall,
                   w_sem, send, recv):
    heads, batch, head_dim = o_ref.shape
    half = heads // 2
    cols = part.shape[2]
    rows = batch // PIECES
    sp, y = lax.axis_index('sp'), lax.axis_index('tp')
    c, x = lax.rem(sp, 2), sp // 2
    to_c, to_x, to_y = {'sp': sp + 1 - 2 * c}, {'sp': sp + 2 - 4 * x}, {'tp': 1 - y}
    block = lambda xx, cc, yy: 4 * xx + 2 * cc + yy
    mine = block(x, c, y)

    barrier = pltpu.get_barrier_semaphore()
    for dev in (to_c, to_x, to_y):
        pl.semaphore_signal(barrier, inc=1, device_id=dev, device_id_type=MESH)

    w_copies = [pltpu.make_async_copy(w_hbm.at[:, pl.ds(pl.multiple_of((2 * sp + h) * cols, cols), cols)], w.at[h], w_sem.at[h]) for h in range(2)]
    hid_copy = pltpu.make_async_copy(hid_hbm.at[:, pl.ds(pl.multiple_of(mine * cols, cols), cols)], hid, w_sem.at[2])
    hid_copy.start()
    for cp in w_copies:
        cp.start()
    pl.semaphore_wait(barrier, 3)

    def copy(kind, j, src, dst, dev):
        return pltpu.make_async_remote_copy(src_ref=src, dst_ref=dst, send_sem=send.at[kind, j], recv_sem=recv.at[kind, j], device_id=dev, device_id_type=MESH)

    def at(j):
        return pl.ds(j * rows, rows)

    pending = []

    def push(cp):
        cp.start()
        pending.append(cp)

    stat_c = copy(0, 0, st_ref, st1, to_c)
    push(stat_c)
    o_copies = [copy(1, j, o_ref.at[pl.ds((1 - c) * half, half), at(j)], r1.at[:, at(j)], to_c) for j in range(PIECES)]
    for cp in o_copies:
        push(cp)

    def pick_half(a):
        return jnp.where(c == 0, a[:, :half], a[:, half:])

    stat_c.wait_recv()
    m_a, l_a, m_b, l_b = (pick_half(v) for v in (st_ref[0], st_ref[1], st1[0], st1[1]))
    top = jnp.maximum(m_a, m_b)
    f_a, f_b = jnp.exp2(m_a - top), jnp.exp2(m_b - top)
    stc[0] = top
    stc[1] = l_a * f_a + l_b * f_b
    stat_x = copy(2, 0, stc, st2, to_x)
    push(stat_x)
    x_copies = [copy(3, j, c1.at[:, at(j)], r2.at[:, at(j)], to_x) for j in range(PIECES)]
    for j in range(PIECES):
        o_copies[j].wait_recv()
        lo = j * rows
        for h in range(half):
            c1[h, at(j)] = o_ref[c * half + h, at(j)] * f_a[lo:lo + rows, h:h + 1] + r1[h, at(j)] * f_b[lo:lo + rows, h:h + 1]
        push(x_copies[j])

    stat_x.wait_recv()
    m_a, l_a, m_b, l_b = stc[0], stc[1], st2[0], st2[1]
    top = jnp.maximum(m_a, m_b)
    g_a, g_b = jnp.exp2(m_a - top), jnp.exp2(m_b - top)
    inv = 1.0 / (l_a * g_a + l_b * g_b)
    g_a, g_b = g_a * inv, g_b * inv

    own_att = att.at[pl.ds(c * half, half)]
    att_copies = [copy(4, j, own_att.at[:, at(j)], own_att.at[:, at(j)], to_c) for j in range(PIECES)]
    part_copies = [copy(5, j, part.at[1 - y, at(j)], r3.at[at(j)], to_y) for j in range(PIECES)]

    def spread(kind, j, blk, dev):
        return copy(kind, j, yall.at[blk, at(j)], yall.at[blk, at(j)], dev)

    b_x, b_y, b_xy = block(1 - x, c, y), block(x, c, 1 - y), block(1 - x, c, 1 - y)

    def finish_heads(j):
        x_copies[j].wait_recv()
        lo = j * rows
        for h in range(half):
            att[c * half + h, at(j)] = c1[h, at(j)] * g_a[lo:lo + rows, h:h + 1] + r2[h, at(j)] * g_b[lo:lo + rows, h:h + 1]
        push(att_copies[j])

    def multiply(j):
        if j == 0:
            for cp in w_copies:
                cp.wait()
        att_copies[j].wait_recv()
        for h in range(heads):
            lhs[:, h * head_dim:(h + 1) * head_dim] = att[h, at(j)].astype(jnp.bfloat16)

        def tiles(side):
            def tile(n, carry):
                sl = pl.ds(pl.multiple_of(n * 256, 256), 256)
                part[side, at(j), sl] = jnp.dot(lhs[...], w[side, :, sl], preferred_element_type=jnp.float32)
                return carry
            lax.fori_loop(0, cols // 256, tile, 0)

        tiles(1 - y)
        push(part_copies[j])
        tiles(y)

    def finish_sum(j):
        if j == 0:
            hid_copy.wait()
        part_copies[j].wait_recv()
        yall[mine, at(j)] = hid[at(j)].astype(jnp.float32) + (part[y, at(j)] + r3[at(j)])
        push(spread(7, j, mine, to_x))
        push(spread(8, j, mine, to_y))
        push(spread(6, j, mine, to_c))

    def forward(j):
        spread(7, j, b_x, to_x).wait_recv()
        push(spread(10, j, b_x, to_y))
        push(spread(9, j, b_x, to_c))
        spread(8, j, b_y, to_y).wait_recv()
        push(spread(11, j, b_y, to_c))

    def forward_last(j):
        spread(10, j, b_xy, to_y).wait_recv()
        push(spread(12, j, b_xy, to_c))

    def emit(j):
        spread(6, j, block(x, 1 - c, y), to_c).wait_recv()
        spread(9, j, block(1 - x, 1 - c, y), to_c).wait_recv()
        spread(11, j, block(x, 1 - c, 1 - y), to_c).wait_recv()
        spread(12, j, block(1 - x, 1 - c, 1 - y), to_c).wait_recv()
        for g in range(8):
            y_ref[at(j), g * cols:(g + 1) * cols] = yall[g, at(j)].astype(y_ref.dtype)

    stages = ((finish_heads, 0), (finish_sum, 1), (multiply, 0), (forward, 2), (forward_last, 3), (emit, 4))
    for t in range(PIECES + 4):
        for stage, lag in stages:
            if 0 <= t - lag < PIECES:
                stage(t - lag)
    for cp in pending:
        cp.wait_send()


def combine_and_project(o, stats, w_o, hidden):
    heads, batch, head_dim = o.shape
    cols = w_o.shape[1] // 8
    half = heads // 2
    f32 = jnp.float32
    return pl.pallas_call(
        combine_kernel,
        out_shape=jax.ShapeDtypeStruct(hidden.shape, hidden.dtype),
        in_specs=[VMEM, VMEM, ANY, ANY],
        out_specs=VMEM,
        scratch_shapes=[
            pltpu.VMEM((2, w_o.shape[0], cols), w_o.dtype),
            pltpu.VMEM((batch, cols), hidden.dtype),
            pltpu.VMEM((half, batch, head_dim), f32),
            pltpu.VMEM(stats.shape, f32),
            pltpu.VMEM((half, batch, head_dim), f32),
            pltpu.VMEM((2, batch, half), f32),
            pltpu.VMEM((half, batch, head_dim), f32),
            pltpu.VMEM((2, batch, half), f32),
            pltpu.VMEM((heads, batch, head_dim), f32),
            pltpu.VMEM((batch // PIECES, heads * head_dim), jnp.bfloat16),
            pltpu.VMEM((2, batch, cols), f32),
            pltpu.VMEM((batch, cols), f32),
            pltpu.VMEM((8, batch, cols), f32),
            pltpu.SemaphoreType.DMA((3,)),
            pltpu.SemaphoreType.DMA((13, PIECES)),
            pltpu.SemaphoreType.DMA((13, PIECES)),
        ],
        compiler_params=pltpu.CompilerParams(collective_id=1, has_side_effects=True, vmem_limit_bytes=56 * 1024 * 1024),
        name='combine',
    )(o, stats, w_o, hidden)


def project(hidden, lengths, norm_gain, w_q, w_k, w_v, inv_freq):
    batch_size = hidden.shape[0]
    head_dim = 2 * inv_freq.shape[0]
    normed = rms_norm(hidden, norm_gain)
    q_heads = jnp.dot(normed, w_q, preferred_element_type=jnp.float32).astype(jnp.bfloat16).reshape(batch_size, -1, head_dim)
    k_new = jnp.dot(normed, w_k, preferred_element_type=jnp.float32).astype(jnp.bfloat16).reshape(batch_size, -1, head_dim)
    v_new = jnp.dot(normed, w_v, preferred_element_type=jnp.float32).astype(jnp.bfloat16).reshape(batch_size, -1, head_dim)
    angles = lengths.astype(jnp.float32)[:, None] * inv_freq[None, :]
    q = apply_rope(q_heads, angles).astype(jnp.float32)
    k = apply_rope(k_new, angles).astype(jnp.float32)
    v = v_new.astype(jnp.float32)
    h = q.shape[1] // 2
    g = k.shape[1] // 2
    q_all = jnp.stack([q[:, :h], q[:, h:]])
    kv_all = jnp.stack([jnp.concatenate([k[:, :g], v[:, :g]], 1), jnp.concatenate([k[:, g:], v[:, g:]], 1)])
    return q_all, kv_all


def device_step(hidden, lengths, k_cache, v_cache, norm_gain, w_q, w_k, w_v, w_o, inv_freq):
    q_all, kv_all = project(hidden, lengths, norm_gain, w_q, w_k, w_v, inv_freq)
    k_upd, v_upd, o, stats = write_and_attend(lengths, q_all, kv_all, k_cache, v_cache)
    y_out = combine_and_project(o, stats, w_o, hidden)
    return y_out, k_upd, v_upd


def solution(mesh):
    cache_spec = P('dp', 'sp', 'tp', None)
    in_specs = (P('dp', None), P('dp'), cache_spec, cache_spec, P(None), P(None, 'tp'), P(None, 'tp'), P(None, 'tp'), P('tp', None), P(None))
    out_specs = (P('dp', None), cache_spec, cache_spec)
    return jax.shard_map(device_step, mesh=mesh, in_specs=in_specs, out_specs=out_specs, check_vma=False)
```

time: 365 us -> 159 us (0.44)
  waiting for transfers between devices: 140 us -> 0 us
  Pallas kernels: 0 us -> 111 us
  local copies, waits for them, and re-layouts: 81.1 us -> 5.59 us
  matrix products: 93.9 us -> 33.5 us
  blocking collectives: 18.2 us -> 0 us
  between operations: 14.2 us -> 0.77 us
  other arithmetic: 17 us -> 8.33 us
    pallas_call x0 -> x2, Pallas kernels: none -> 111 us  [the longest x1 62.8 us: combine_and_project(): pl.pallas_call(combine_kernel, out_shape=jax.ShapeDtypeStruct(hidden.shap...]
    psum x1 -> x0, waiting for transfers between devices: 102 us -> none  [device_step(): lax.psum(jnp.dot(attn_out, w_o, preferred_element_type=jnp.float32), 'tp')]
    dot_general x6 -> x3, matrix products: 93.9 us -> 33.5 us  [the longest x1 24.2 us: project(): jnp.dot(normed, w_q, preferred_element_type=jnp.float32)]
    unnamed x11 -> x6, local copies, waits for them, and re-layouts: 48.7 us -> 5.06 us
    all_gather x1 -> x0, waiting for transfers between devices: 37.4 us -> none  [device_step(): all_out = lax.all_gather(part_out, 'sp')]
    scatter x2 -> x0, local copies, waits for them, and re-layouts: 31.6 us -> none  [the longest x1 15.8 us: write_and_attend(): v_upd = v_cache.at[row_ids, write_pos].set(v_new, mode='drop')]
    all_gather x2 -> x0, blocking collectives: 18.2 us -> none  [the longest x1 10.1 us: device_step(): all_sum = lax.all_gather(part_sum, 'sp')]
    reduce_sum x3 -> x0, other arithmetic: 9.08 us -> none  [the longest x1 5.64 us: device_step(): weighted = jnp.sum(factor[..., None] * all_out, axis=0)]
  transfers between devices with their start and end apart: 2 -> 0, of which waited for: 2 -> 0; matrix products, arithmetic and copies ran while one was open for 1% -> 0% of each run, Pallas kernels for 0% -> 0%
where the time goes in v1:
time: 159 us
  Pallas kernels  111 us (70%)
  matrix products  33.5 us (21%)
  other arithmetic  8.33 us (5%)
  local copies, waits for them, and re-layouts  5.59 us (4%)
    pallas_call x1, Pallas kernels, combine_and_project(): pl.pallas_call(combine_kernel, out_shape=jax.ShapeDtypeStruct(hidden.shap...  62.8 us
    pallas_call x1, Pallas kernels, write_and_attend(): pl.pallas_call(attend_kernel, out_shape=out_shape, in_specs=[SMEM, VMEM,...  47.7 us
    dot_general x1, matrix products, project(): jnp.dot(normed, w_q, preferred_element_type=jnp.float32)  24.2 us
    unnamed x6, local copies, waits for them, and re-layouts  5.06 us
    dot_general x1, matrix products, project(): jnp.dot(normed, w_k, preferred_element_type=jnp.float32)  4.69 us
    dot_general x1, matrix products, project(): jnp.dot(normed, w_v, preferred_element_type=jnp.float32)  4.69 us

profile of v1, /device:TPU:0, one launch (start us, length us, event | category | flops | bytes accessed | tf_op | source)
XLA Modules:
  0.0 158.7 jit_solution(8886693483440730059)
XLA Ops:
  0.6 0.0 copy-start
  0.7 0.8 convert_element_type.53
  1.5 2.1 %fusion.1 = f32[128]{0:T(128)S(1)} fusion(bf16[128,8192]{1,0:T(8,128)(2,1)} %hid_hbm.1), kind=kLoop, calls=%fused_computation.4 | loop fusion | flops 3145600 | bytes 2097664 | tf_op jit(solution)/shard_map/reduce_sum | solution.py:20
  3.6 0.7 convert_element_type.48
  4.3 0.3 multiply_cosine_fusion
  4.6 4.7 %fusion.6 = f32[128,512]{1,0:T(8,128)S(1)} fusion(bf16[8192,512]{1,0:T(8,128)(2,1)} %param.16, bf16[128,8192]{1,0:T(8,128)(2,1)S(1)} %copy-done, f32[8192]{0:T(1024)S(1)} %convert_element_type.48, f32[128]{0:T(128)S(1)} %add_rsqrt_fusion), kind=kOutput, calls=%fused_computation.14 | convolution fusion | flops 1078067200 | bytes 10781184 | tf_op jit(solution)/shard_map/dot_general | solution.py:352
  9.3 0.1 reshape.84
  9.4 0.3 subtract_convert_fusion.1
  9.7 0.2 maximum_convert_fusion.1
  9.9 0.1 fusion.10
  10.0 4.7 %fusion.5 = f32[128,512]{1,0:T(8,128)S(1)} fusion(bf16[8192,512]{1,0:T(8,128)(2,1)} %param.17, bf16[128,8192]{1,0:T(8,128)(2,1)S(1)} %copy-done, f32[8192]{0:T(1024)S(1)} %convert_element_type.48, f32[128]{0:T(128)S(1)} %add_rsqrt_fusion), kind=kOutput, calls=%fused_computation.12 | convolution fusion | flops 1078067200 | bytes 10781184 | tf_op jit(solution)/shard_map/dot_general | solution.py:353
  14.7 0.1 reshape.85
  14.8 0.1 fusion.11
  14.9 0.2 maximum_bitcast_fusion
  15.1 0.9 pad_maximum_fusion.1.kv_ref
  16.1 24.2 %fusion.4 = f32[16,8,32,128]{3,1,2,0:T(8,128)} fusion(bf16[8192,4096]{1,0:T(8,128)(2,1)} %param.15, bf16[128,8192]{1,0:T(8,128)(2,1)S(1)} %copy-done, f32[8192]{0:T(1024)S(1)} %convert_element_type.48, f32[128]{0:T(128)S(1)} %add_rsqrt_fusion), kind=kOutput, calls=%fused_computation.10 | convolution fusion | flops 8595177472 | bytes 71336448 | tf_op jit(solution)/shard_map/dot_general | solution.py:351
  40.2 2.0 %copy.13 = f32[16,8,32,128]{3,2,1,0:T(8,128)S(1)} copy(f32[16,8,32,128]{3,1,2,0:T(8,128)} %fusion.4) | data formatting | bytes 4194304
  42.2 0.8 subtract_convert_fusion
  43.0 0.5 maximum_convert_fusion
  43.5 0.1 slice_bitcast_fusion.1
  43.7 1.5 pad_maximum_fusion.q_ref
  45.1 47.7 %attend.1 = (bf16[128,1024,128]{2,1,0:T(8,128)(2,1)}, bf16[128,1024,128]{2,1,0:T(8,128)(2,1)}, f32[32,128,128]{2,1,0:T(8,128)}, f32[2,128,32]{2,1,0:T(8,128)}) custom-call(s32[128]{0:T(128)} %len_ref.1, f32[2,128,16,128]{3,2,1,0:T(8,128)} %pad_maximum_fusion.q_ref, f32[2,128,4,128]{3,2,1,0:T(4,128)} %pad_maximum_fusion.1.kv_ref, ...), custom_call_target="tpu_custom_call" | custom-call | flops 2147483648 | bytes 134217728 | tf_op jit(solution)/shard_map/attend/pallas_call | solution.py:150
  92.8 62.8 %combine.1 = bf16[128,8192]{1,0:T(8,128)(2,1)} custom-call(f32[32,128,128]{2,1,0:T(8,128)} %get-tuple-element.7.o_ref, f32[2,128,32]{2,1,0:T(8,128)} %get-tuple-element.8.st_ref, bf16[4096,8192]{1,0:T(8,128)(2,1)} %w_hbm.1, bf16[128,8192]{1,0:T(8,128)(2,1)} %hid_hbm.1), custom_call_target="tpu_custom_call" | custom-call | tf_op jit(solution)/shard_map/combine/pallas_call | solution.py:319
  155.6 3.1 %copy.15 = bf16[128,8192]{1,0:T(8,128)(2,1)} copy(bf16[128,8192]{1,0:T(8,128)(2,1)} %combine.1) | data formatting | bytes 4194304
  (4 shorter events, 0.0 us)
Async XLA Ops:
  0.6 4.0 %copy-start = (bf16[128,8192]{1,0:T(8,128)(2,1)S(1)}, bf16[128,8192]{1,0:T(8,128)(2,1)}, u32[]{:S(2)}) copy-start(bf16[128,8192]{1,0:T(8,128)(2,1)} %hid_hbm.1) | copy-start | bytes 6291460
  0.6 3.6 %copy-start.1 = (f32[64]{0:T(128)S(1)}, f32[64]{0:T(128)}, u32[]{:S(2)}) copy-start(f32[64]{0:T(128)} %param.19) | copy-start | bytes 772

commit v2 on v1

v2 whole, which is shorter than its diff:
```python
import functools

import jax
import jax.numpy as jnp
from jax import lax
from jax.experimental import pallas as pl
from jax.experimental.pallas import tpu as pltpu
from jax.sharding import PartitionSpec as P

NORM_EPS = 1e-5
NEG_BIG = -3.0e38
LOG2E = 1.4426950408889634
ANY = pl.BlockSpec(memory_space=pl.ANY)
VMEM = pl.BlockSpec(memory_space=pltpu.VMEM)
SMEM = pl.BlockSpec(memory_space=pltpu.SMEM)


CHUNK = 8
NBUF = 6
LAG = 3


def attend_kernel(first, count, len_ref, q_ref, kv_ref, k_hbm, v_hbm, *refs):
    ko_hbm, vo_hbm, own_ref, oth_ref, kbuf, vbuf, obuf, mbuf, lbuf, in_sem, out_sem = refs[-11:]
    batch, rows, head_dim = k_hbm.shape
    kv_local = kv_ref.shape[2]
    heads = q_ref.shape[0] * q_ref.shape[2]
    slots = rows // kv_local
    steps = count // CHUNK
    slot_start = lax.axis_index('sp') * slots

    def copies_in(i):
        b = lax.rem(i, NBUF)
        src = pl.ds(first + i * CHUNK, CHUNK)
        return (pltpu.make_async_copy(k_hbm.at[src], kbuf.at[b], in_sem.at[0, b]),
                pltpu.make_async_copy(v_hbm.at[src], vbuf.at[b], in_sem.at[1, b]))

    def copies_out(i):
        b = lax.rem(i, NBUF)
        dst = pl.ds(first + i * CHUNK, CHUNK)
        return (pltpu.make_async_copy(kbuf.at[b], ko_hbm.at[dst], out_sem.at[0, b]),
                pltpu.make_async_copy(vbuf.at[b], vo_hbm.at[dst], out_sem.at[1, b]))

    for i in range(NBUF - LAG):
        for c in copies_in(i):
            c.start()

    col = lax.broadcasted_iota(jnp.int32, (heads, rows), 1)
    row = lax.broadcasted_iota(jnp.int32, (heads, rows), 0)
    head_ok = lax.rem(col, kv_local) == row // (heads // kv_local)
    tile_slot = lax.broadcasted_iota(jnp.int32, (16, head_dim), 0) // kv_local
    lane = lax.broadcasted_iota(jnp.int32, (heads, batch), 1)
    score_scale = head_dim ** -0.5 * LOG2E
    half = heads // 2
    core = lax.rem(lax.axis_index('sp'), 2)

    def step(i, carry):
        buf = lax.rem(i, NBUF)

        @pl.when((i >= LAG) & (i + NBUF - LAG < steps))
        def _():
            for c in copies_out(i - LAG):
                c.wait()

        @pl.when(i + NBUF - LAG < steps)
        def _():
            for c in copies_in(i + NBUF - LAG):
                c.start()

        for c in copies_in(i):
            c.wait()
        for s in range(CHUNK):
            b = first + i * CHUNK + s
            pos = len_ref[b] - slot_start
            own = (pos >= 0) & (pos < slots)
            safe = jnp.where(own, pos, 0)
            per_tile = 16 // kv_local
            base = pl.multiple_of(safe // per_tile * 16, 16)
            pick = (tile_slot == lax.rem(safe, per_tile)) & own
            for dst, which in ((kbuf, 0), (vbuf, 1)):
                new = jnp.concatenate([kv_ref[which, b]] * per_tile, axis=0)
                old = dst[buf, s, pl.ds(base, 16), :].astype(jnp.float32)
                dst[buf, s, pl.ds(base, 16), :] = jnp.where(pick, new, old).astype(jnp.bfloat16)
        m_all, l_all = mbuf[...], lbuf[...]
        for s in range(0, CHUNK, 2):
            b0 = first + i * CHUNK + s
            b1 = b0 + 1
            limit0 = (len_ref[b0] - slot_start + 1) * kv_local
            limit1 = (len_ref[b1] - slot_start + 1) * kv_local
            q0 = jnp.concatenate([q_ref[0, b0], q_ref[1, b0]], axis=0).astype(jnp.bfloat16)
            q1 = jnp.concatenate([q_ref[0, b1], q_ref[1, b1]], axis=0).astype(jnp.bfloat16)
            zero = jnp.zeros_like(q0)
            q = jnp.concatenate([jnp.concatenate([q0, zero], axis=1), jnp.concatenate([zero, q1], axis=1)], axis=0)
            k = jnp.concatenate([kbuf[buf, s], kbuf[buf, s + 1]], axis=1)
            v = jnp.concatenate([vbuf[buf, s], vbuf[buf, s + 1]], axis=1)
            scores = lax.dot_general(q, k, (((1,), (1,)), ((), ())), preferred_element_type=jnp.float32)
            valid = jnp.concatenate([head_ok & (col < limit0), head_ok & (col < limit1)], axis=0)
            scores = jnp.where(valid, scores * score_scale, NEG_BIG)
            top = jnp.max(scores, axis=-1, keepdims=True)
            weights = jnp.where(valid, jnp.exp2(scores - top), 0.0)
            total = jnp.sum(weights, axis=-1, keepdims=True)
            out = jnp.dot(weights.astype(jnp.bfloat16), v, preferred_element_type=jnp.float32)
            obuf[s] = out[:heads, :head_dim]
            obuf[s + 1] = out[heads:, head_dim:]
            m_all = jnp.where(lane == b0, top[:heads], jnp.where(lane == b1, top[heads:], m_all))
            l_all = jnp.where(lane == b0, total[:heads], jnp.where(lane == b1, total[heads:], l_all))
        mbuf[...] = m_all
        lbuf[...] = l_all
        out_rows = pl.ds(pl.multiple_of(i * CHUNK, CHUNK), CHUNK)
        by_head = jnp.swapaxes(obuf[...], 0, 1)
        own_ref[:half, out_rows] = jnp.where(core == 0, by_head[:half], by_head[half:])
        oth_ref[:half, out_rows] = jnp.where(core == 0, by_head[half:], by_head[:half])
        for c in copies_out(i):
            c.start()

        return carry

    mbuf[...] = jnp.zeros_like(mbuf)
    lbuf[...] = jnp.zeros_like(lbuf)
    lax.fori_loop(0, steps, step, 0)
    for i in range(steps - NBUF, steps):
        for c in copies_out(i):
            c.wait()
    stats = []
    for lo in (0, half):
        rows_ml = [mbuf[lo:lo + half], lbuf[lo:lo + half], jnp.zeros((batch - 2 * half, batch), jnp.float32)]
        stats.append(jnp.concatenate(rows_ml, axis=0).T[first:first + count])
    own_ref[half] = jnp.where(core == 0, stats[0], stats[1])
    oth_ref[half] = jnp.where(core == 0, stats[1], stats[0])


def write_and_attend(first, count, lengths, q_all, kv_all, k_cache, v_cache, written=()):
    batch, rows, head_dim = k_cache.shape
    heads = q_all.shape[0] * q_all.shape[2]
    part = jax.ShapeDtypeStruct((heads // 2 + 1, count, head_dim), jnp.float32)
    cache = jax.ShapeDtypeStruct(k_cache.shape, k_cache.dtype)
    return pl.pallas_call(
        functools.partial(attend_kernel, first, count),
        out_shape=(cache, cache, part, part),
        in_specs=[SMEM, VMEM, VMEM, ANY, ANY] + [ANY] * len(written),
        out_specs=(ANY, ANY, VMEM, VMEM),
        input_output_aliases={5: 0, 6: 1} if written else {},
        scratch_shapes=[
            pltpu.VMEM((NBUF, CHUNK, rows, head_dim), jnp.bfloat16),
            pltpu.VMEM((NBUF, CHUNK, rows, head_dim), jnp.bfloat16),
            pltpu.VMEM((CHUNK, heads, head_dim), jnp.float32),
            pltpu.VMEM((heads, batch), jnp.float32),
            pltpu.VMEM((heads, batch), jnp.float32),
            pltpu.SemaphoreType.DMA((2, NBUF)),
            pltpu.SemaphoreType.DMA((2, NBUF)),
        ],
        compiler_params=pltpu.CompilerParams(vmem_limit_bytes=34 * 1024 * 1024),
        cost_estimate=pl.CostEstimate(flops=100 * count * heads * rows * head_dim, bytes_accessed=8 * count * rows * head_dim, transcendentals=0),
        name='attend',
    )(lengths, q_all, kv_all, k_cache, v_cache, *written)


FIRST = 64
B_PIECES = 2
MESH = pl.DeviceIdType.MESH


def weigh(tiles):
    half = 16
    tops = [t[:, :half] for t in tiles]
    top = functools.reduce(jnp.maximum, tops)
    scales = [jnp.exp2(m - top) for m in tops]
    total = sum(t[:, half:2 * half] * s for t, s in zip(tiles, scales))
    return top, total, scales


def combine_kernel(own_a, core_a, x_a, diag_a, own_b, oth_b, w_hbm, hid_hbm, y_ref, w, hid, r1, c1, r2, att, lhs, part, r3, yall,
                   w_sem, send, recv):
    heads, batch, head_dim = att.shape
    half = heads // 2
    cols = part.shape[2]
    first = own_a.shape[1]
    piece_rows = own_b.shape[1] // B_PIECES
    pieces = [(0, first)] + [(first + j * piece_rows, piece_rows) for j in range(B_PIECES)]
    sp, y = lax.axis_index('sp'), lax.axis_index('tp')
    c, x = lax.rem(sp, 2), sp // 2
    to_c, to_x, to_y = {'sp': sp + 1 - 2 * c}, {'sp': sp + 2 - 4 * x}, {'tp': 1 - y}
    block = lambda xx, cc, yy: 4 * xx + 2 * cc + yy
    mine = block(x, c, y)

    barrier = pltpu.get_barrier_semaphore()
    for dev in (to_c, to_x, to_y):
        pl.semaphore_signal(barrier, inc=1, device_id=dev, device_id_type=MESH)

    w_copies = [pltpu.make_async_copy(w_hbm.at[:, pl.ds(pl.multiple_of((2 * sp + h) * cols, cols), cols)], w.at[h], w_sem.at[h]) for h in range(2)]
    hid_copy = pltpu.make_async_copy(hid_hbm.at[:, pl.ds(pl.multiple_of(mine * cols, cols), cols)], hid, w_sem.at[2])
    hid_copy.start()
    for cp in w_copies:
        cp.start()
    pl.semaphore_wait(barrier, 3)

    def copy(kind, j, src, dst, dev):
        return pltpu.make_async_remote_copy(src_ref=src, dst_ref=dst, send_sem=send.at[kind, j], recv_sem=recv.at[kind, j], device_id=dev, device_id_type=MESH)

    def at(j):
        return pl.ds(*pieces[j])

    def local(j):
        return pl.ds(pieces[j][0] - first, pieces[j][1])

    pending = []

    def push(cp):
        cp.start()
        pending.append(cp)

    b_range = range(1, B_PIECES + 1)
    stat_c = copy(0, 0, oth_b.at[half], r1.at[half], to_c)
    push(stat_c)
    o_copies = {j: copy(1, j, oth_b.at[pl.ds(0, half), local(j)], r1.at[pl.ds(0, half), local(j)], to_c) for j in b_range}
    for j in b_range:
        push(o_copies[j])

    own_att = att.at[pl.ds(c * half, half)]
    att_copies = [copy(4, j, own_att.at[:, at(j)], own_att.at[:, at(j)], to_c) for j in range(B_PIECES + 1)]
    part_copies = [copy(5, j, part.at[1 - y, at(j)], r3.at[at(j)], to_y) for j in range(B_PIECES + 1)]

    parts_a = (own_a, core_a, x_a, diag_a)
    _, total, scales = weigh([p[half] for p in parts_a])
    scales = [s / total for s in scales]
    for h in range(half):
        att[c * half + h, at(0)] = sum(p[h] * s[:, h:h + 1] for p, s in zip(parts_a, scales))
    push(att_copies[0])

    stat_c.wait_recv()
    top, total, scales = weigh([own_b[half], r1[half]])
    c1[half] = jnp.concatenate([top, total, jnp.zeros((own_b.shape[1], head_dim - 2 * half), jnp.float32)], axis=1)
    stat_x = copy(2, 0, c1.at[half], r2.at[half], to_x)
    push(stat_x)
    x_copies = {j: copy(3, j, c1.at[pl.ds(0, half), local(j)], r2.at[pl.ds(0, half), local(j)], to_x) for j in b_range}
    for j in b_range:
        o_copies[j].wait_recv()
        lo, n = pieces[j][0] - first, pieces[j][1]
        for h in range(half):
            c1[h, local(j)] = own_b[h, local(j)] * scales[0][lo:lo + n, h:h + 1] + r1[h, local(j)] * scales[1][lo:lo + n, h:h + 1]
        push(x_copies[j])

    def spread(kind, j, blk, dev):
        return copy(kind, j, yall.at[blk, at(j)], yall.at[blk, at(j)], dev)

    b_x, b_y, b_xy = block(1 - x, c, y), block(x, c, 1 - y), block(1 - x, c, 1 - y)
    final = {}

    def finish_heads(j):
        if j == 0:
            return
        if j == 1:
            stat_x.wait_recv()
            _, tot, sc = weigh([c1[half], r2[half]])
            final['scales'] = [s / tot for s in sc]
        x_copies[j].wait_recv()
        lo, n = pieces[j][0] - first, pieces[j][1]
        for h in range(half):
            att[c * half + h, at(j)] = sum(p[h, local(j)] * s[lo:lo + n, h:h + 1] for p, s in zip((c1, r2), final['scales']))
        push(att_copies[j])

    def multiply(j):
        if j == 0:
            for cp in w_copies:
                cp.wait()
        att_copies[j].wait_recv()
        n = pieces[j][1]
        for h in range(heads):
            lhs[:n, h * head_dim:(h + 1) * head_dim] = att[h, at(j)].astype(jnp.bfloat16)

        def tiles(side):
            def tile(i, carry):
                sl = pl.ds(pl.multiple_of(i * 256, 256), 256)
                part[side, at(j), sl] = jnp.dot(lhs[:n], w[side, :, sl], preferred_element_type=jnp.float32)
                return carry
            lax.fori_loop(0, cols // 256, tile, 0)

        tiles(1 - y)
        push(part_copies[j])
        tiles(y)

    def finish_sum(j):
        if j == 0:
            hid_copy.wait()
        part_copies[j].wait_recv()
        yall[mine, at(j)] = hid[at(j)].astype(jnp.float32) + (part[y, at(j)] + r3[at(j)])
        push(spread(8, j, mine, to_y))
        push(spread(7, j, mine, to_x))
        push(spread(6, j, mine, to_c))

    def forward(j):
        def from_x():
            spread(7, j, b_x, to_x).wait_recv()
            if j:
                push(spread(10, j, b_x, to_y))
            push(spread(9, j, b_x, to_c))

        def from_y():
            spread(8, j, b_y, to_y).wait_recv()
            if not j:
                push(spread(10, j, b_y, to_x))
            push(spread(11, j, b_y, to_c))

        for take in (from_x, from_y) if j else (from_y, from_x):
            take()

    def forward_last(j):
        spread(10, j, b_xy, to_y).wait_recv()
        push(spread(12, j, b_xy, to_c))

    def emit(j):
        spread(6, j, block(x, 1 - c, y), to_c).wait_recv()
        spread(9, j, block(1 - x, 1 - c, y), to_c).wait_recv()
        spread(11, j, block(x, 1 - c, 1 - y), to_c).wait_recv()
        spread(12, j, block(1 - x, 1 - c, 1 - y), to_c).wait_recv()
        for g in range(8):
            y_ref[at(j), g * cols:(g + 1) * cols] = yall[g, at(j)].astype(y_ref.dtype)

    stages = ((finish_heads, 0), (finish_sum, 1), (multiply, 0), (forward, 2), (forward_last, 3), (emit, 4))
    for t in range(len(pieces) + 4):
        for stage, lag in stages:
            if 0 <= t - lag < len(pieces):
                stage(t - lag)
    for cp in pending:
        cp.wait_send()


def combine_and_project(parts_a, parts_b, w_o, hidden):
    ext, nb_a, head_dim = parts_a[0].shape
    nb_b = parts_b[0].shape[1]
    batch = nb_a + nb_b
    half = ext - 1
    heads = 2 * half
    cols = w_o.shape[1] // 8
    f32 = jnp.float32
    kinds, count = 13, B_PIECES + 1
    return pl.pallas_call(
        combine_kernel,
        out_shape=jax.ShapeDtypeStruct(hidden.shape, hidden.dtype),
        in_specs=[VMEM] * 6 + [ANY, ANY],
        out_specs=VMEM,
        scratch_shapes=[
            pltpu.VMEM((2, w_o.shape[0], cols), w_o.dtype),
            pltpu.VMEM((batch, cols), hidden.dtype),
            pltpu.VMEM((ext, nb_b, head_dim), f32),
            pltpu.VMEM((ext, nb_b, head_dim), f32),
            pltpu.VMEM((ext, nb_b, head_dim), f32),
            pltpu.VMEM((heads, batch, head_dim), f32),
            pltpu.VMEM((max(nb_a, nb_b // B_PIECES), heads * head_dim), jnp.bfloat16),
            pltpu.VMEM((2, batch, cols), f32),
            pltpu.VMEM((batch, cols), f32),
            pltpu.VMEM((8, batch, cols), f32),
            pltpu.SemaphoreType.DMA((3,)),
            pltpu.SemaphoreType.DMA((kinds, count)),
            pltpu.SemaphoreType.DMA((kinds, count)),
        ],
        compiler_params=pltpu.CompilerParams(collective_id=1, has_side_effects=True, vmem_limit_bytes=38 * 1024 * 1024),
        name='combine',
    )(*parts_a, *parts_b, w_o, hidden)


K_PIECES = 8
N_TILE = 1024
AHEAD = 5


def project_kernel(hid_hbm, gain_ref, len_ref, freq_ref, wq_hbm, wk_hbm, wv_hbm, q_ref, kv_ref, hid_ref, cos_ref, sin_ref, gain32, normed, acc, kv_acc, wbuf, kv_buf, hid_sem, w_sem, send, recv):
    batch, depth = hid_ref.shape
    head_dim = cos_ref.shape[1]
    q_cols = wq_hbm.shape[1] // 2
    kv_cols = wk_hbm.shape[1]
    k_rows = depth // K_PIECES
    q_tiles = q_cols // N_TILE
    sp = lax.axis_index('sp')
    c = lax.rem(sp, 2)
    to_c = {'sp': sp + 1 - 2 * c}

    barrier = pltpu.get_barrier_semaphore()
    pl.semaphore_signal(barrier, inc=1, device_id=to_c, device_id_type=MESH)

    def fetch(n, k):
        rows = pl.ds(k * k_rows, k_rows)
        if n == q_tiles:
            return tuple(pltpu.make_async_copy(src.at[rows], kv_buf.at[k], w_sem.at[n, k]) for src in (wk_hbm, wv_hbm))
        col = pl.ds(pl.multiple_of(c * q_cols + n * N_TILE, N_TILE), N_TILE)
        return (pltpu.make_async_copy(wq_hbm.at[rows, col], wbuf.at[n, k], w_sem.at[n, k]),)

    def start(n, k):
        cps = fetch(n, k)
        if n < q_tiles:
            cps[0].start()
            return
        for core in range(2):
            @pl.when(c == core)
            def _(core=core):
                cps[core].start()

    hid_copy = pltpu.make_async_copy(hid_hbm, hid_ref, hid_sem)
    hid_copy.start()
    order = [piece for k in range(K_PIECES) for piece in ((0, k), (q_tiles, k))]
    order += [(n, k) for n in range(1, q_tiles) for k in range(K_PIECES)]
    for piece in order[:AHEAD]:
        start(*piece)

    def angle_tables():
        angles = jnp.broadcast_to(len_ref[...].astype(jnp.float32), (batch, batch)).T[:, :head_dim] * jnp.concatenate([freq_ref[...]] * 2, axis=1)
        sin_ang = jnp.sin(angles)
        cos_ref[...] = jnp.cos(angles)
        sin_ref[...] = jnp.where(lax.broadcasted_iota(jnp.int32, angles.shape, 1) < head_dim // 2, -sin_ang, sin_ang)

    gain32[...] = gain_ref[...].astype(jnp.float32)
    hid_copy.wait()
    step = 1024
    total = jnp.zeros((batch, 1), jnp.float32)
    for j in range(depth // step):
        part = hid_ref[:, j * step:(j + 1) * step].astype(jnp.float32)
        total = total + jnp.sum(part * part, axis=-1, keepdims=True)
    inv_rms = lax.rsqrt(total / depth + NORM_EPS)
    lanes = gain_ref.shape[1]

    def normalize(k):
        for j in range(k * k_rows // lanes, (k + 1) * k_rows // lanes):
            sl = slice(j * lanes, (j + 1) * lanes)
            normed[:, sl] = (hid_ref[:, sl].astype(jnp.float32) * inv_rms * gain32[j:j + 1, :]).astype(normed.dtype)

    def round_bf16(v):
        return v.astype(jnp.bfloat16).astype(jnp.float32)

    def rope(v):
        return round_bf16(v * cos_ref[...] + pltpu.roll(v, head_dim // 2, 1) * sin_ref[...])

    sends = []

    def push(slot, ref, index):
        cp = pltpu.make_async_remote_copy(src_ref=ref.at[index], dst_ref=ref.at[index], send_sem=send.at[slot], recv_sem=recv.at[slot], device_id=to_c, device_id_type=MESH)
        if not sends:
            pl.semaphore_wait(barrier, 1)
        cp.start()
        sends.append(cp)

    per = N_TILE // head_dim

    def epilogue_kv():
        for h in range(kv_cols // head_dim):
            v = round_bf16(kv_acc[:, h * head_dim:(h + 1) * head_dim])
            kv_ref[c, :, h, :] = jnp.where(c == 0, rope(v), v)
        push(q_tiles, kv_ref, c)

    def epilogue(n):
        for h in range(per):
            q_ref[c, :, n * per + h, :] = rope(round_bf16(acc[n % 2, :, h * head_dim:(h + 1) * head_dim]))
        push(n, q_ref, (c, slice(None), pl.ds(n * per, per)))

    for i, (n, k) in enumerate(order):
        fetch(n, k)[0].wait()
        if i + AHEAD < len(order):
            start(*order[i + AHEAD])
        if n == 0:
            normalize(k)
        lhs = normed[:, k * k_rows:(k + 1) * k_rows]
        if n == q_tiles:
            prod = jnp.dot(lhs, kv_buf[k], preferred_element_type=jnp.float32)
            kv_acc[...] = prod + kv_acc[...] if k else prod
        else:
            prod = jnp.dot(lhs, wbuf[n, k], preferred_element_type=jnp.float32)
            acc[n % 2] = prod + acc[n % 2] if k else prod
        if (n, k) == (0, 3):
            angle_tables()
        if (n, k) == (1, 1):
            epilogue_kv()
        if 0 < n < q_tiles and k == 2:
            epilogue(n - 1)
    epilogue(q_tiles - 1)
    for cp in sends:
        cp.wait()


def project(hidden, lengths, norm_gain, w_q, w_k, w_v, inv_freq):
    batch, depth = hidden.shape
    head_dim = 2 * inv_freq.shape[0]
    q_heads = w_q.shape[1] // 2 // head_dim
    kv_heads = w_k.shape[1] // head_dim
    q_tiles = w_q.shape[1] // 2 // N_TILE
    return pl.pallas_call(
        project_kernel,
        out_shape=(jax.ShapeDtypeStruct((2, batch, q_heads, head_dim), jnp.float32), jax.ShapeDtypeStruct((2, batch, kv_heads, head_dim), jnp.float32)),
        in_specs=[ANY, VMEM, VMEM, VMEM, ANY, ANY, ANY],
        out_specs=(VMEM, VMEM),
        scratch_shapes=[
            pltpu.VMEM((batch, depth), hidden.dtype),
            pltpu.VMEM((batch, head_dim), jnp.float32),
            pltpu.VMEM((batch, head_dim), jnp.float32),
            pltpu.VMEM((depth // 128, 128), jnp.float32),
            pltpu.VMEM((batch, depth), jnp.bfloat16),
            pltpu.VMEM((2, batch, N_TILE), jnp.float32),
            pltpu.VMEM((batch, w_k.shape[1]), jnp.float32),
            pltpu.VMEM((q_tiles, K_PIECES, depth // K_PIECES, N_TILE), w_q.dtype),
            pltpu.VMEM((K_PIECES, depth // K_PIECES, w_k.shape[1]), w_k.dtype),
            pltpu.SemaphoreType.DMA,
            pltpu.SemaphoreType.DMA((q_tiles + 1, K_PIECES)),
            pltpu.SemaphoreType.DMA((q_tiles + 1,)),
            pltpu.SemaphoreType.DMA((q_tiles + 1,)),
        ],
        compiler_params=pltpu.CompilerParams(collective_id=0, has_side_effects=True, vmem_limit_bytes=53 * 1024 * 1024),
        name='project',
    )(hidden, norm_gain.reshape(depth // 128, 128), lengths.reshape(1, batch), inv_freq.reshape(1, head_dim // 2), w_q, w_k, w_v)


def device_step(hidden, lengths, k_cache, v_cache, norm_gain, w_q, w_k, w_v, w_o, inv_freq):
    batch, slots, kv_local, head_dim = k_cache.shape
    q_all, kv_all = project(hidden, lengths, norm_gain, w_q, w_k, w_v, inv_freq)
    flat = (batch, slots * kv_local, head_dim)
    shared = (lengths, q_all, kv_all, k_cache.reshape(flat), v_cache.reshape(flat))
    k_upd, v_upd, own_a, oth_a = write_and_attend(0, FIRST, *shared)
    swap = lambda array, flip: lax.ppermute(array, 'sp', [(s, s ^ flip) for s in range(4)])
    parts_a = (own_a, swap(oth_a, 1), swap(own_a, 2), swap(oth_a, 3))
    k_upd, v_upd, own_b, oth_b = write_and_attend(FIRST, batch - FIRST, *shared, written=(k_upd, v_upd))
    y_out = combine_and_project(parts_a, (own_b, oth_b), w_o, hidden)
    return y_out, k_upd.reshape(k_cache.shape), v_upd.reshape(v_cache.shape)


def solution(mesh):
    cache_spec = P('dp', 'sp', 'tp', None)
    in_specs = (P('dp', None), P('dp'), cache_spec, cache_spec, P(None), P(None, 'tp'), P(None, 'tp'), P(None, 'tp'), P('tp', None), P(None))
    out_specs = (P('dp', None), cache_spec, cache_spec)
    return jax.shard_map(device_step, mesh=mesh, in_specs=in_specs, out_specs=out_specs, check_vma=False)
```

time: 159 us -> 123 us (0.77)
  matrix products: 33.5 us -> 0 us
  other arithmetic: 8.33 us -> 0 us
  starting transfers between devices: 0 us -> 3.05 us
  Pallas kernels: 111 us -> 114 us
    dot_general x3 -> x0, matrix products: 33.5 us -> none  [the longest x1 24.2 us: project(): jnp.dot(normed, w_q, preferred_element_type=jnp.float32)]
    pallas_call x1 -> x3, Pallas kernels: 47.7 us -> 68.9 us  [the longest x2 49.3 us: write_and_attend(): pl.pallas_call(functools.partial(attend_kernel, first, count), out_shape=...]
    pallas_call x1, Pallas kernels: 62.8 us -> 45.4 us  [combine_and_project(): pl.pallas_call(combine_kernel, out_shape=jax.ShapeDtypeStruct(hidden.shap...]
    another operation x5 -> x0, other arithmetic: 3.71 us -> none  [the longest x1 1.46 us: project(): q_all = jnp.stack([q[:, :h], q[:, h:]])]
    ppermute x0 -> x3, starting transfers between devices: none -> 3.05 us  [device_step(): lax.ppermute(array, 'sp', [(s, s ^ flip) for s in range(4)])]
    convert_element_type x4 -> x0, other arithmetic: 2.23 us -> none  [the longest x1 0.81 us: project(): angles = lengths.astype(jnp.float32)[:, None] * inv_freq[None, :]]
    reduce_sum x1 -> x0, other arithmetic: 2.08 us -> none  [rms_norm(): jnp.mean(hidden_f32 * hidden_f32, axis=-1, keepdims=True) + NORM_EPS]
    unnamed x6 -> x11, local copies, waits for them, and re-layouts: 5.06 us -> 4.93 us
  transfers between devices with their start and end apart: 0 -> 3, of which waited for: 0 -> 0; matrix products, arithmetic and copies ran while one was open for 0% -> 0% of each run, Pallas kernels for 0% -> 20%
where the time goes in v2:
time: 123 us
  Pallas kernels  114 us (93%)
  local copies, waits for them, and re-layouts  4.93 us (4%)
  starting transfers between devices  3.05 us (2%)
    pallas_call x2, Pallas kernels, write_and_attend(): pl.pallas_call(functools.partial(attend_kernel, first, count), out_shape=...  49.3 us
    pallas_call x1, Pallas kernels, combine_and_project(): pl.pallas_call(combine_kernel, out_shape=jax.ShapeDtypeStruct(hidden.shap...  45.4 us
    pallas_call x1, Pallas kernels, project(): pl.pallas_call(project_kernel, out_shape=(jax.ShapeDtypeStruct((2, batch,...  19.6 us
    unnamed x11, local copies, waits for them, and re-layouts  4.93 us
    ppermute x3, starting transfers between devices, device_step(): lax.ppermute(array, 'sp', [(s, s ^ flip) for s in range(4)])  3.05 us
  transfers between devices with their start and end apart: 3, of which 0 were waited for; matrix products, arithmetic and copies ran while one was open for 0% of the time, Pallas kernels for 20%

profile of v2, /device:TPU:0, one launch (start us, length us, event | category | flops | bytes accessed | tf_op | source)
XLA Modules:
  0.0 123.1 jit_solution(17697571391186777367)
XLA Ops:
  0.6 0.0 copy-start.2
  0.6 0.7 copy-done.2
  1.4 0.0 copy-start.3
  1.4 0.7 copy-done.3
  2.0 0.0 copy-start.4
  2.0 0.7 copy-done.4
  2.7 19.6 %project.1 = (f32[2,128,16,128]{3,2,1,0:T(8,128)}, f32[2,128,4,128]{3,2,1,0:T(4,128)S(1)}) custom-call(bf16[128,8192]{1,0:T(8,128)(2,1)} %hid_hbm.3, bf16[64,128]{1,0:T(8,128)(2,1)S(1)} %bitcast.7, s32[1,128]{1,0:T(1,128)S(1)} %bitcast.8, f32[1,64]{1,0:T(1,128)S(1)} %bitcast.9, bf16[8192,4096]{1,0:T(8,128)(2,1)} %wq_hbm.1, bf16[8192,512]{1,0:T(8,128)(2,1)} %wk_hbm.1, ...), custom_call_target="tpu_custom_call" | custom-call | tf_op jit(solution)/shard_map/project/pallas_call | solution.py:484
  22.3 0.0 copy-start.1
  22.3 1.6 %copy-done.1 = f32[2,128,16,128]{3,2,1,0:T(8,128)S(1)} copy-done((f32[2,128,16,128]{3,2,1,0:T(8,128)S(1)}, f32[2,128,16,128]{3,2,1,0:T(8,128)}, u32[]{:S(2)}) %copy-start.1) | copy-done | bytes 2097176
  23.9 24.6 %attend.2 = (bf16[128,1024,128]{2,1,0:T(8,128)(2,1)}, bf16[128,1024,128]{2,1,0:T(8,128)(2,1)}, f32[17,64,128]{2,1,0:T(8,128)S(1)}, f32[17,64,128]{2,1,0:T(8,128)S(1)}) custom-call(s32[128]{0:T(128)S(1)} %copy-done.3, f32[2,128,16,128]{3,2,1,0:T(8,128)S(1)} %copy-done.1, f32[2,128,4,128]{3,2,1,0:T(4,128)S(1)} %get-tuple-element.14.kv_ref, ...), custom_call_target="tpu_custom_call" | custom-call | flops 26843545600 | bytes 67108864 | tf_op jit(solution)/shard_map/attend/pallas_call | solution.py:137
  48.5 2.6 %collective-permute-start.2 = (f32[17,64,128]{2,1,0:T(8,128)S(1)}, f32[17,64,128]{2,1,0:T(8,128)S(1)}, u32[]{:S(2)}, u32[]{:S(2)}) collective-permute-start(f32[17,64,128]{2,1,0:T(8,128)S(1)} %get-tuple-element.16), channel_id=1, source_target_pairs={{0,3},{1,2},{2,1},{3,0},{4,7},{5,6},{6,5},{7,4}} | collective-permute-start | bytes 1671176 | tf_op jit(solution)/shard_map/ppermute | solution.py:515
  51.1 0.1 collective-permute-start
  51.2 0.3 collective-permute-start.1
  51.5 0.0 copy-start
  51.5 24.7 %attend.3 = (bf16[128,1024,128]{2,1,0:T(8,128)(2,1)}, bf16[128,1024,128]{2,1,0:T(8,128)(2,1)}, f32[17,64,128]{2,1,0:T(8,128)S(1)}, f32[17,64,128]{2,1,0:T(8,128)S(1)}) custom-call(s32[128]{0:T(128)S(1)} %copy-done.3, f32[2,128,16,128]{3,2,1,0:T(8,128)S(1)} %copy-done.1, ...), custom_call_target="tpu_custom_call", output_to_operand_aliasing={{0}: (5, {}), {1}: (6, {})} | custom-call | flops 26843545600 | bytes 67108864 | tf_op jit(solution)/shard_map/attend/pallas_call | solution.py:137
  76.3 0.0 collective-permute-done.1.x_a
  76.3 0.0 collective-permute-done.2.diag_a
  76.3 0.0 collective-permute-done.core_a
  76.3 0.0 copy-done
  76.3 45.4 %combine.1 = bf16[128,8192]{1,0:T(8,128)(2,1)S(1)} custom-call(f32[17,64,128]{2,1,0:T(8,128)S(1)} %get-tuple-element.15.own_a, f32[17,64,128]{2,1,0:T(8,128)S(1)} %collective-permute-done.core_a, f32[17,64,128]{2,1,0:T(8,128)S(1)} %collective-permute-done.1.x_a, f32[17,64,128]{2,1,0:T(8,128)S(1)} %collective-permute-done.2.diag_a, ...), custom_call_target="tpu_custom_call" | custom-call | tf_op jit(solution)/shard_map/combine/pallas_call | solution.py:337
  121.7 1.3 %copy.18 = bf16[128,8192]{1,0:T(8,128)(2,1)} copy(bf16[128,8192]{1,0:T(8,128)(2,1)S(1)} %combine.1) | data formatting | bytes 4194304
Async XLA Ops:
  0.6 0.7 copy-start.2
  1.4 0.7 copy-start.3
  2.0 0.7 copy-start.4
  22.3 1.6 %copy-start.1 = (f32[2,128,16,128]{3,2,1,0:T(8,128)S(1)}, f32[2,128,16,128]{3,2,1,0:T(8,128)}, u32[]{:S(2)}) copy-start(f32[2,128,16,128]{3,2,1,0:T(8,128)} %get-tuple-element.13.q_ref) | copy-start | bytes 6291460
  48.5 27.8 %collective-permute-start.2 = (f32[17,64,128]{2,1,0:T(8,128)S(1)}, f32[17,64,128]{2,1,0:T(8,128)S(1)}, u32[]{:S(2)}, u32[]{:S(2)}) collective-permute-start(f32[17,64,128]{2,1,0:T(8,128)S(1)} %get-tuple-element.16), channel_id=1, source_target_pairs={{0,3},{1,2},{2,1},{3,0},{4,7},{5,6},{6,5},{7,4}} | collective-permute-start | bytes 1671176 | tf_op jit(solution)/shard_map/ppermute | solution.py:515
  51.1 25.2 %collective-permute-start = (f32[17,64,128]{2,1,0:T(8,128)S(1)}, f32[17,64,128]{2,1,0:T(8,128)S(1)}, u32[]{:S(2)}, u32[]{:S(2)}) collective-permute-start(f32[17,64,128]{2,1,0:T(8,128)S(1)} %get-tuple-element.16), channel_id=1, source_target_pairs={{0,1},{1,0},{2,3},{3,2},{4,5},{5,4},{6,7},{7,6}} | collective-permute-start | bytes 1671176 | tf_op jit(solution)/shard_map/ppermute | solution.py:515
  51.2 25.0 %collective-permute-start.1 = (f32[17,64,128]{2,1,0:T(8,128)S(1)}, f32[17,64,128]{2,1,0:T(8,128)S(1)}, u32[]{:S(2)}, u32[]{:S(2)}) collective-permute-start(f32[17,64,128]{2,1,0:T(8,128)S(1)} %get-tuple-element.15.own_a), channel_id=1, source_target_pairs={{0,2},{1,3},{2,0},{3,1},{4,6},{5,7},{6,4},{7,5}} | collective-permute-start | bytes 1671176 | tf_op jit(solution)/shard_map/ppermute | solution.py:515
  51.5 24.7 %copy-start = (bf16[128,8192]{1,0:T(8,128)(2,1)S(1)}, bf16[128,8192]{1,0:T(8,128)(2,1)}, u32[]{:S(2)}) copy-start(bf16[128,8192]{1,0:T(8,128)(2,1)} %hid_hbm.3) | copy-start | bytes 6291460

commit v3 on v2

--- a/solution.py
+++ b/solution.py
@@ -11,39 +11,48 @@
 NEG_BIG = -3.0e38
 LOG2E = 1.4426950408889634
 ANY = pl.BlockSpec(memory_space=pl.ANY)
+HBM = pl.BlockSpec(memory_space=pltpu.HBM)
 VMEM = pl.BlockSpec(memory_space=pltpu.VMEM)
 SMEM = pl.BlockSpec(memory_space=pltpu.SMEM)
 
 
 CHUNK = 8
-NBUF = 6
-LAG = 3
-
-
-def attend_kernel(first, count, len_ref, q_ref, kv_ref, k_hbm, v_hbm, *refs):
-    ko_hbm, vo_hbm, own_ref, oth_ref, kbuf, vbuf, obuf, mbuf, lbuf, in_sem, out_sem = refs[-11:]
+PART = 4
+NBUF = 5
+LAG = 2
+
+
+def attend_kernel(first, count, len_ref, q_hbm, kv_hbm, k_hbm, v_hbm, *refs):
+    ko_hbm, vo_hbm, own_ref, oth_ref, q_ref, kv_ref, kbuf, vbuf, obuf, mbuf, lbuf, in_sem, out_sem, q_sem = refs[-14:]
     batch, rows, head_dim = k_hbm.shape
     kv_local = kv_ref.shape[2]
-    heads = q_ref.shape[0] * q_ref.shape[2]
+    heads = 2 * q_ref.shape[2]
     slots = rows // kv_local
     steps = count // CHUNK
     slot_start = lax.axis_index('sp') * slots
 
-    def copies_in(i):
+    def copies_in(i, part):
         b = lax.rem(i, NBUF)
-        src = pl.ds(first + i * CHUNK, CHUNK)
-        return (pltpu.make_async_copy(k_hbm.at[src], kbuf.at[b], in_sem.at[0, b]),
-                pltpu.make_async_copy(v_hbm.at[src], vbuf.at[b], in_sem.at[1, b]))
-
-    def copies_out(i):
+        src = pl.ds(first + i * CHUNK + part * PART, PART)
+        dst = pl.ds(part * PART, PART)
+        return (pltpu.make_async_copy(k_hbm.at[src], kbuf.at[b, dst], in_sem.at[0, b, part]),
+                pltpu.make_async_copy(v_hbm.at[src], vbuf.at[b, dst], in_sem.at[1, b, part]))
+
+    def copies_out(i, part):
         b = lax.rem(i, NBUF)
-        dst = pl.ds(first + i * CHUNK, CHUNK)
-        return (pltpu.make_async_copy(kbuf.at[b], ko_hbm.at[dst], out_sem.at[0, b]),
-                pltpu.make_async_copy(vbuf.at[b], vo_hbm.at[dst], out_sem.at[1, b]))
-
+        src = pl.ds(part * PART, PART)
+        dst = pl.ds(first + i * CHUNK + part * PART, PART)
+        return (pltpu.make_async_copy(kbuf.at[b, src], ko_hbm.at[dst], out_sem.at[0, b, part]),
+                pltpu.make_async_copy(vbuf.at[b, src], vo_hbm.at[dst], out_sem.at[1, b, part]))
+
+    parts = range(CHUNK // PART)
+    small = (pltpu.make_async_copy(q_hbm.at[:, pl.ds(first, count)], q_ref, q_sem.at[0]), pltpu.make_async_copy(kv_hbm.at[:, pl.ds(first, count)], kv_ref, q_sem.at[1]))
+    for cp in small:
+        cp.start()
     for i in range(NBUF - LAG):
-        for c in copies_in(i):
-            c.start()
+        for part in parts:
+            for cp in copies_in(i, part):
+                cp.start()
 
     col = lax.broadcasted_iota(jnp.int32, (heads, rows), 1)
     row = lax.broadcasted_iota(jnp.int32, (heads, rows), 0)
@@ -54,73 +63,85 @@
     half = heads // 2
     core = lax.rem(lax.axis_index('sp'), 2)
 
+    def store_token(i, s):
+        buf = lax.rem(i, NBUF)
+        b = first + i * CHUNK + s
+        pos = len_ref[b] - slot_start
+        own = (pos >= 0) & (pos < slots)
+        safe = jnp.where(own, pos, 0)
+        per_tile = 16 // kv_local
+        base = pl.multiple_of(safe // per_tile * 16, 16)
+        pick = (tile_slot == lax.rem(safe, per_tile)) & own
+        for dst, which in ((kbuf, 0), (vbuf, 1)):
+            new = jnp.concatenate([kv_ref[which, b - first]] * per_tile, axis=0)
+            old = dst[buf, s, pl.ds(base, 16), :].astype(jnp.float32)
+            dst[buf, s, pl.ds(base, 16), :] = jnp.where(pick, new, old).astype(jnp.bfloat16)
+
+    def attend_pair(i, s, m_all, l_all):
+        buf = lax.rem(i, NBUF)
+        b0 = first + i * CHUNK + s
+        b1 = b0 + 1
+        limit0 = (len_ref[b0] - slot_start + 1) * kv_local
+        limit1 = (len_ref[b1] - slot_start + 1) * kv_local
+        q0 = jnp.concatenate([q_ref[0, b0 - first], q_ref[1, b0 - first]], axis=0).astype(jnp.bfloat16)
+        q1 = jnp.concatenate([q_ref[0, b1 - first], q_ref[1, b1 - first]], axis=0).astype(jnp.bfloat16)
+        zero = jnp.zeros_like(q0)
+        q = jnp.concatenate([jnp.concatenate([q0, zero], axis=1), jnp.concatenate([zero, q1], axis=1)], axis=0)
+        k = jnp.concatenate([kbuf[buf, s], kbuf[buf, s + 1]], axis=1)
+        v = jnp.concatenate([vbuf[buf, s], vbuf[buf, s + 1]], axis=1)
+        scores = lax.dot_general(q, k, (((1,), (1,)), ((), ())), preferred_element_type=jnp.float32)
+        valid = jnp.concatenate([head_ok & (col < limit0), head_ok & (col < limit1)], axis=0)
+        scores = jnp.where(valid, scores * score_scale, NEG_BIG)
+        top = jnp.max(scores, axis=-1, keepdims=True)
+        weights = jnp.where(valid, jnp.exp2(scores - top), 0.0)
+        total = jnp.sum(weights, axis=-1, keepdims=True)
+        out = jnp.dot(weights.astype(jnp.bfloat16), v, preferred_element_type=jnp.float32)
+        obuf[s] = out[:heads, :head_dim]
+        obuf[s + 1] = out[heads:, head_dim:]
+        m_all = jnp.where(lane == b0, top[:heads], jnp.where(lane == b1, top[heads:], m_all))
+        l_all = jnp.where(lane == b0, total[:heads], jnp.where(lane == b1, total[heads:], l_all))
+        return m_all, l_all
+
     def step(i, carry):
-        buf = lax.rem(i, NBUF)
-
-        @pl.when((i >= LAG) & (i + NBUF - LAG < steps))
-        def _():
-            for c in copies_out(i - LAG):
-                c.wait()
-
-        @pl.when(i + NBUF - LAG < steps)
-        def _():
-            for c in copies_in(i + NBUF - LAG):
-                c.start()
-
-        for c in copies_in(i):
-            c.wait()
-        for s in range(CHUNK):
-            b = first + i * CHUNK + s
-            pos = len_ref[b] - slot_start
-            own = (pos >= 0) & (pos < slots)
-            safe = jnp.where(own, pos, 0)
-            per_tile = 16 // kv_local
-            base = pl.multiple_of(safe // per_tile * 16, 16)
-            pick = (tile_slot == lax.rem(safe, per_tile)) & own
-            for dst, which in ((kbuf, 0), (vbuf, 1)):
-                new = jnp.concatenate([kv_ref[which, b]] * per_tile, axis=0)
-                old = dst[buf, s, pl.ds(base, 16), :].astype(jnp.float32)
-                dst[buf, s, pl.ds(base, 16), :] = jnp.where(pick, new, old).astype(jnp.bfloat16)
+        for part in parts:
+            @pl.when((i >= LAG) & (i + NBUF - LAG < steps))
+            def _():
+                for cp in copies_out(i - LAG, part):
+                    cp.wait()
+
+            @pl.when(i + NBUF - LAG < steps)
+            def _():
+                for cp in copies_in(i + NBUF - LAG, part):
+                    cp.start()
+
         m_all, l_all = mbuf[...], lbuf[...]
-        for s in range(0, CHUNK, 2):
-            b0 = first + i * CHUNK + s
-            b1 = b0 + 1
-            limit0 = (len_ref[b0] - slot_start + 1) * kv_local
-            limit1 = (len_ref[b1] - slot_start + 1) * kv_local
-            q0 = jnp.concatenate([q_ref[0, b0], q_ref[1, b0]], axis=0).astype(jnp.bfloat16)
-            q1 = jnp.concatenate([q_ref[0, b1], q_ref[1, b1]], axis=0).astype(jnp.bfloat16)
-            zero = jnp.zeros_like(q0)
-            q = jnp.concatenate([jnp.concatenate([q0, zero], axis=1), jnp.concatenate([zero, q1], axis=1)], axis=0)
-            k = jnp.concatenate([kbuf[buf, s], kbuf[buf, s + 1]], axis=1)
-            v = jnp.concatenate([vbuf[buf, s], vbuf[buf, s + 1]], axis=1)
-            scores = lax.dot_general(q, k, (((1,), (1,)), ((), ())), preferred_element_type=jnp.float32)
-            valid = jnp.concatenate([head_ok & (col < limit0), head_ok & (col < limit1)], axis=0)
-            scores = jnp.where(valid, scores * score_scale, NEG_BIG)
-            top = jnp.max(scores, axis=-1, keepdims=True)
-            weights = jnp.where(valid, jnp.exp2(scores - top), 0.0)
-            total = jnp.sum(weights, axis=-1, keepdims=True)
-            out = jnp.dot(weights.astype(jnp.bfloat16), v, preferred_element_type=jnp.float32)
-            obuf[s] = out[:heads, :head_dim]
-            obuf[s + 1] = out[heads:, head_dim:]
-            m_all = jnp.where(lane == b0, top[:heads], jnp.where(lane == b1, top[heads:], m_all))
-            l_all = jnp.where(lane == b0, total[:heads], jnp.where(lane == b1, total[heads:], l_all))
+        for part in parts:
+            for cp in copies_in(i, part):
+                cp.wait()
+            for s in range(part * PART, (part + 1) * PART):
+                store_token(i, s)
+            for s in range(part * PART, (part + 1) * PART, 2):
+                m_all, l_all = attend_pair(i, s, m_all, l_all)
+            for cp in copies_out(i, part):
+                cp.start()
         mbuf[...] = m_all
         lbuf[...] = l_all
         out_rows = pl.ds(pl.multiple_of(i * CHUNK, CHUNK), CHUNK)
         by_head = jnp.swapaxes(obuf[...], 0, 1)
         own_ref[:half, out_rows] = jnp.where(core == 0, by_head[:half], by_head[half:])
         oth_ref[:half, out_rows] = jnp.where(core == 0, by_head[half:], by_head[:half])
-        for c in copies_out(i):
-            c.start()
 
         return carry
 
     mbuf[...] = jnp.zeros_like(mbuf)
     lbuf[...] = jnp.zeros_like(lbuf)
+    for cp in small:
+        cp.wait()
     lax.fori_loop(0, steps, step, 0)
     for i in range(steps - NBUF, steps):
-        for c in copies_out(i):
-            c.wait()
+        for part in parts:
+            for cp in copies_out(i, part):
+                cp.wait()
     stats = []
     for lo in (0, half):
         rows_ml = [mbuf[lo:lo + half], lbuf[lo:lo + half], jnp.zeros((batch - 2 * half, batch), jnp.float32)]
@@ -137,17 +158,20 @@
     return pl.pallas_call(
         functools.partial(attend_kernel, first, count),
         out_shape=(cache, cache, part, part),
-        in_specs=[SMEM, VMEM, VMEM, ANY, ANY] + [ANY] * len(written),
+        in_specs=[SMEM] + [HBM] * 4 + [ANY] * len(written),
         out_specs=(ANY, ANY, VMEM, VMEM),
         input_output_aliases={5: 0, 6: 1} if written else {},
         scratch_shapes=[
+            pltpu.VMEM((2, count) + q_all.shape[2:], jnp.float32),
+            pltpu.VMEM((2, count) + kv_all.shape[2:], jnp.float32),
             pltpu.VMEM((NBUF, CHUNK, rows, head_dim), jnp.bfloat16),
             pltpu.VMEM((NBUF, CHUNK, rows, head_dim), jnp.bfloat16),
             pltpu.VMEM((CHUNK, heads, head_dim), jnp.float32),
             pltpu.VMEM((heads, batch), jnp.float32),
             pltpu.VMEM((heads, batch), jnp.float32),
-            pltpu.SemaphoreType.DMA((2, NBUF)),
-            pltpu.SemaphoreType.DMA((2, NBUF)),
+            pltpu.SemaphoreType.DMA((2, NBUF, CHUNK // PART)),
+            pltpu.SemaphoreType.DMA((2, NBUF, CHUNK // PART)),
+            pltpu.SemaphoreType.DMA((2,)),
         ],
         compiler_params=pltpu.CompilerParams(vmem_limit_bytes=34 * 1024 * 1024),
         cost_estimate=pl.CostEstimate(flops=100 * count * heads * rows * head_dim, bytes_accessed=8 * count * rows * head_dim, transcendentals=0),
@@ -156,7 +180,9 @@
 
 
 FIRST = 64
-B_PIECES = 2
+PIECES = (64, 48, 16)
+MODES = 'QPD'
+LAGS = (0, 1, 0, 2, 3, 4)
 MESH = pl.DeviceIdType.MESH
 
 
@@ -175,8 +201,8 @@
     half = heads // 2
     cols = part.shape[2]
     first = own_a.shape[1]
-    piece_rows = own_b.shape[1] // B_PIECES
-    pieces = [(0, first)] + [(first + j * piece_rows, piece_rows) for j in range(B_PIECES)]
+    pieces = [(sum(PIECES[:j]), n) for j, n in enumerate(PIECES)]
+    count = len(pieces)
     sp, y = lax.axis_index('sp'), lax.axis_index('tp')
     c, x = lax.rem(sp, 2), sp // 2
     to_c, to_x, to_y = {'sp': sp + 1 - 2 * c}, {'sp': sp + 2 - 4 * x}, {'tp': 1 - y}
@@ -188,8 +214,7 @@
         pl.semaphore_signal(barrier, inc=1, device_id=dev, device_id_type=MESH)
 
     w_copies = [pltpu.make_async_copy(w_hbm.at[:, pl.ds(pl.multiple_of((2 * sp + h) * cols, cols), cols)], w.at[h], w_sem.at[h]) for h in range(2)]
-    hid_copy = pltpu.make_async_copy(hid_hbm.at[:, pl.ds(pl.multiple_of(mine * cols, cols), cols)], hid, w_sem.at[2])
-    hid_copy.start()
+    w_copies += [pltpu.make_async_copy(hid_hbm.at[:, pl.ds(pl.multiple_of((2 * sp + h) * cols, cols), cols)], hid.at[h], w_sem.at[2 + h]) for h in range(2)]
     for cp in w_copies:
         cp.start()
     pl.semaphore_wait(barrier, 3)
@@ -209,7 +234,7 @@
         cp.start()
         pending.append(cp)
 
-    b_range = range(1, B_PIECES + 1)
+    b_range = range(1, count)
     stat_c = copy(0, 0, oth_b.at[half], r1.at[half], to_c)
     push(stat_c)
     o_copies = {j: copy(1, j, oth_b.at[pl.ds(0, half), local(j)], r1.at[pl.ds(0, half), local(j)], to_c) for j in b_range}
@@ -217,8 +242,8 @@
         push(o_copies[j])
 
     own_att = att.at[pl.ds(c * half, half)]
-    att_copies = [copy(4, j, own_att.at[:, at(j)], own_att.at[:, at(j)], to_c) for j in range(B_PIECES + 1)]
-    part_copies = [copy(5, j, part.at[1 - y, at(j)], r3.at[at(j)], to_y) for j in range(B_PIECES + 1)]
+    att_copies = [copy(4, j, own_att.at[:, at(j)], own_att.at[:, at(j)], to_c) for j in range(count)]
+    part_copies = [copy(5, j, part.at[1 - y, at(j)], r3.at[1 - y, at(j)], to_y) for j in range(count)]
 
     parts_a = (own_a, core_a, x_a, diag_a)
     _, total, scales = weigh([p[half] for p in parts_a])
@@ -278,12 +303,24 @@
         tiles(1 - y)
         push(part_copies[j])
         tiles(y)
+        if MODES[j] == 'D':
+            push(both_copy(j))
+
+    def both_copy(j):
+        return copy(13, j, part.at[y, at(j)], r3.at[y, at(j)], to_y)
 
     def finish_sum(j):
-        if j == 0:
-            hid_copy.wait()
         part_copies[j].wait_recv()
-        yall[mine, at(j)] = hid[at(j)].astype(jnp.float32) + (part[y, at(j)] + r3[at(j)])
+        if MODES[j] == 'D':
+            both_copy(j).wait_recv()
+            for side in range(2):
+                yall[block(x, c, side), at(j)] = hid[side, at(j)].astype(jnp.float32) + (part[side, at(j)] + r3[side, at(j)])
+            push(spread(7, j, mine, to_x))
+            push(spread(10, j, b_y, to_x))
+            push(spread(6, j, mine, to_c))
+            push(spread(11, j, b_y, to_c))
+            return
+        yall[mine, at(j)] = hid[y, at(j)].astype(jnp.float32) + (part[y, at(j)] + r3[y, at(j)])
         push(spread(8, j, mine, to_y))
         push(spread(7, j, mine, to_x))
         push(spread(6, j, mine, to_c))
@@ -291,17 +328,17 @@
     def forward(j):
         def from_x():
             spread(7, j, b_x, to_x).wait_recv()
-            if j:
+            if MODES[j] == 'P':
                 push(spread(10, j, b_x, to_y))
             push(spread(9, j, b_x, to_c))
 
         def from_y():
             spread(8, j, b_y, to_y).wait_recv()
-            if not j:
+            if MODES[j] == 'Q':
                 push(spread(10, j, b_y, to_x))
             push(spread(11, j, b_y, to_c))
 
-        for take in (from_x, from_y) if j else (from_y, from_x):
+        for take in {'P': (from_x, from_y), 'Q': (from_y, from_x), 'D': (from_x,)}[MODES[j]]:
             take()
 
     def forward_last(j):
@@ -316,10 +353,10 @@
         for g in range(8):
             y_ref[at(j), g * cols:(g + 1) * cols] = yall[g, at(j)].astype(y_ref.dtype)
 
-    stages = ((finish_heads, 0), (finish_sum, 1), (multiply, 0), (forward, 2), (forward_last, 3), (emit, 4))
-    for t in range(len(pieces) + 4):
+    stages = tuple(zip((finish_heads, finish_sum, multiply, forward, forward_last, emit), LAGS))
+    for t in range(count + max(LAGS)):
         for stage, lag in stages:
-            if 0 <= t - lag < len(pieces):
+            if 0 <= t - lag < count:
                 stage(t - lag)
     for cp in pending:
         cp.wait_send()
@@ -333,7 +370,7 @@
     heads = 2 * half
     cols = w_o.shape[1] // 8
     f32 = jnp.float32
-    kinds, count = 13, B_PIECES + 1
+    kinds, count = 14, len(PIECES)
     return pl.pallas_call(
         combine_kernel,
         out_shape=jax.ShapeDtypeStruct(hidden.shape, hidden.dtype),
@@ -341,16 +378,16 @@
         out_specs=VMEM,
         scratch_shapes=[
             pltpu.VMEM((2, w_o.shape[0], cols), w_o.dtype),
-            pltpu.VMEM((batch, cols), hidden.dtype),
+            pltpu.VMEM((2, batch, cols), hidden.dtype),
             pltpu.VMEM((ext, nb_b, head_dim), f32),
             pltpu.VMEM((ext, nb_b, head_dim), f32),
             pltpu.VMEM((ext, nb_b, head_dim), f32),
             pltpu.VMEM((heads, batch, head_dim), f32),
-            pltpu.VMEM((max(nb_a, nb_b // B_PIECES), heads * head_dim), jnp.bfloat16),
+            pltpu.VMEM((max(PIECES), heads * head_dim), jnp.bfloat16),
             pltpu.VMEM((2, batch, cols), f32),
-            pltpu.VMEM((batch, cols), f32),
+            pltpu.VMEM((2, batch, cols), f32),
             pltpu.VMEM((8, batch, cols), f32),
-            pltpu.SemaphoreType.DMA((3,)),
+            pltpu.SemaphoreType.DMA((4,)),
             pltpu.SemaphoreType.DMA((kinds, count)),
             pltpu.SemaphoreType.DMA((kinds, count)),
         ],
@@ -361,10 +398,10 @@
 
 K_PIECES = 8
 N_TILE = 1024
-AHEAD = 5
-
-
-def project_kernel(hid_hbm, gain_ref, len_ref, freq_ref, wq_hbm, wk_hbm, wv_hbm, q_ref, kv_ref, hid_ref, cos_ref, sin_ref, gain32, normed, acc, kv_acc, wbuf, kv_buf, hid_sem, w_sem, send, recv):
+AHEAD = 8
+
+
+def project_kernel(hid_hbm, gain_hbm, len_hbm, freq_hbm, wq_hbm, wk_hbm, wv_hbm, q_ref, kv_ref, hid_ref, gain_ref, len_ref, freq_ref, cos_ref, sin_ref, gain32, normed, acc, kv_acc, wbuf, kv_buf, hid_sem, w_sem, send, recv):
     batch, depth = hid_ref.shape
     head_dim = cos_ref.shape[1]
     q_cols = wq_hbm.shape[1] // 2
@@ -395,8 +432,10 @@
             def _(core=core):
                 cps[core].start()
 
-    hid_copy = pltpu.make_async_copy(hid_hbm, hid_ref, hid_sem)
-    hid_copy.start()
+    small = [pltpu.make_async_copy(src, dst, hid_sem.at[i]) for i, (src, dst) in enumerate(
+        ((hid_hbm, hid_ref), (gain_hbm, gain_ref), (len_hbm, len_ref), (freq_hbm, freq_ref)))]
+    for cp in small:
+        cp.start()
     order = [piece for k in range(K_PIECES) for piece in ((0, k), (q_tiles, k))]
     order += [(n, k) for n in range(1, q_tiles) for k in range(K_PIECES)]
     for piece in order[:AHEAD]:
@@ -408,8 +447,9 @@
         cos_ref[...] = jnp.cos(angles)
         sin_ref[...] = jnp.where(lax.broadcasted_iota(jnp.int32, angles.shape, 1) < head_dim // 2, -sin_ang, sin_ang)
 
+    for cp in small:
+        cp.wait()
     gain32[...] = gain_ref[...].astype(jnp.float32)
-    hid_copy.wait()
     step = 1024
     total = jnp.zeros((batch, 1), jnp.float32)
     for j in range(depth // step):
@@ -484,10 +524,13 @@
     return pl.pallas_call(
         project_kernel,
         out_shape=(jax.ShapeDtypeStruct((2, batch, q_heads, head_dim), jnp.float32), jax.ShapeDtypeStruct((2, batch, kv_heads, head_dim), jnp.float32)),
-        in_specs=[ANY, VMEM, VMEM, VMEM, ANY, ANY, ANY],
+        in_specs=[HBM] * 7,
         out_specs=(VMEM, VMEM),
         scratch_shapes=[
             pltpu.VMEM((batch, depth), hidden.dtype),
+            pltpu.VMEM((depth // 128, 128), norm_gain.dtype),
+            pltpu.VMEM((1, batch), jnp.int32),
+            pltpu.VMEM((1, head_dim // 2), jnp.float32),
             pltpu.VMEM((batch, head_dim), jnp.float32),
             pltpu.VMEM((batch, head_dim), jnp.float32),
             pltpu.VMEM((depth // 128, 128), jnp.float32),
@@ -496,12 +539,12 @@
             pltpu.VMEM((batch, w_k.shape[1]), jnp.float32),
             pltpu.VMEM((q_tiles, K_PIECES, depth // K_PIECES, N_TILE), w_q.dtype),
             pltpu.VMEM((K_PIECES, depth // K_PIECES, w_k.shape[1]), w_k.dtype),
-            pltpu.SemaphoreType.DMA,
+            pltpu.SemaphoreType.DMA((4,)),
             pltpu.SemaphoreType.DMA((q_tiles + 1, K_PIECES)),
             pltpu.SemaphoreType.DMA((q_tiles + 1,)),
             pltpu.SemaphoreType.DMA((q_tiles + 1,)),
         ],
-        compiler_params=pltpu.CompilerParams(collective_id=0, has_side_effects=True, vmem_limit_bytes=53 * 1024 * 1024),
+        compiler_params=pltpu.CompilerParams(collective_id=0, has_side_effects=True, vmem_limit_bytes=50 * 1024 * 1024),
         name='project',
     )(hidden, norm_gain.reshape(depth // 128, 128), lengths.reshape(1, batch), inv_freq.reshape(1, head_dim // 2), w_q, w_k, w_v)
 

time: 123 us -> 115 us (0.935)
  Pallas kernels: 114 us -> 107 us
  local copies, waits for them, and re-layouts: 4.93 us -> 3.35 us
    pallas_call x1, Pallas kernels: 45.4 us -> 41.6 us  [combine_and_project(): pl.pallas_call(combine_kernel, out_shape=jax.ShapeDtypeStruct(hidden.shap...]
    pallas_call x1, Pallas kernels: 19.6 us -> 17.3 us  [project(): pl.pallas_call(project_kernel, out_shape=(jax.ShapeDtypeStruct((2, batch,...]
    unnamed x11 -> x9, local copies, waits for them, and re-layouts: 4.93 us -> 3.35 us
  transfers between devices with their start and end apart: 3 -> 3, of which waited for: 0 -> 1; matrix products, arithmetic and copies ran while one was open for 0% -> 0% of each run, Pallas kernels for 20% -> 21%
where the time goes in v3:
time: 115 us
  Pallas kernels  107 us (93%)
  local copies, waits for them, and re-layouts  3.35 us (3%)
  starting transfers between devices  3.04 us (3%)
    pallas_call x2, Pallas kernels, write_and_attend(): pl.pallas_call(functools.partial(attend_kernel, first, count), out_shape=...  48.4 us
    pallas_call x1, Pallas kernels, combine_and_project(): pl.pallas_call(combine_kernel, out_shape=jax.ShapeDtypeStruct(hidden.shap...  41.6 us
    pallas_call x1, Pallas kernels, project(): pl.pallas_call(project_kernel, out_shape=(jax.ShapeDtypeStruct((2, batch,...  17.3 us
    unnamed x9, local copies, waits for them, and re-layouts  3.35 us
    ppermute x3, starting transfers between devices, device_step(): lax.ppermute(array, 'sp', [(s, s ^ flip) for s in range(4)])  3.04 us
  transfers between devices with their start and end apart: 3, of which 1 were waited for; matrix products, arithmetic and copies ran while one was open for 0% of the time, Pallas kernels for 21%

profile of v3, /device:TPU:0, one launch (start us, length us, event | category | flops | bytes accessed | tf_op | source)
XLA Modules:
  0.0 114.8 jit_solution(577719569963990537)
XLA Ops:
  0.6 0.0 copy-start.1
  0.6 0.7 copy-done.1
  1.4 0.0 copy-start.2
  1.4 0.7 copy-done.2
  2.0 0.0 copy-start.3
  2.0 0.7 copy-done.3
  2.7 17.3 %project.1 = (f32[2,128,16,128]{3,2,1,0:T(8,128)S(1)}, f32[2,128,4,128]{3,2,1,0:T(4,128)S(1)}) custom-call(bf16[128,8192]{1,0:T(8,128)(2,1)} %hid_hbm.3, bf16[64,128]{1,0:T(8,128)(2,1)S(1)} %bitcast.7, s32[1,128]{1,0:T(1,128)S(1)} %bitcast.8, f32[1,64]{1,0:T(1,128)S(1)} %bitcast.9, bf16[8192,4096]{1,0:T(8,128)(2,1)} %wq_hbm.1, bf16[8192,512]{1,0:T(8,128)(2,1)} %wk_hbm.1, ...), custom_call_target="tpu_custom_call" | custom-call | tf_op jit(solution)/shard_map/project/pallas_call | solution.py:524
  20.0 24.2 %attend.2 = (bf16[128,1024,128]{2,1,0:T(8,128)(2,1)}, bf16[128,1024,128]{2,1,0:T(8,128)(2,1)}, f32[17,64,128]{2,1,0:T(8,128)S(1)}, f32[17,64,128]{2,1,0:T(8,128)S(1)}) custom-call(s32[128]{0:T(128)S(1)} %copy-done.2, f32[2,128,16,128]{3,2,1,0:T(8,128)S(1)} %get-tuple-element.13.q_hbm, f32[2,128,4,128]{3,2,1,0:T(4,128)S(1)} %get-tuple-element.14.kv_hbm, ...), custom_call_target="tpu_custom_call" | custom-call | flops 26843545600 | bytes 67108864 | tf_op jit(solution)/shard_map/attend/pallas_call | solution.py:158
  44.2 2.6 %collective-permute-start.2 = (f32[17,64,128]{2,1,0:T(8,128)S(1)}, f32[17,64,128]{2,1,0:T(8,128)S(1)}, u32[]{:S(2)}, u32[]{:S(2)}) collective-permute-start(f32[17,64,128]{2,1,0:T(8,128)S(1)} %get-tuple-element.16), channel_id=1, source_target_pairs={{0,3},{1,2},{2,1},{3,0},{4,7},{5,6},{6,5},{7,4}} | collective-permute-start | bytes 1671176 | tf_op jit(solution)/shard_map/ppermute | solution.py:558
  46.8 0.1 collective-permute-start
  46.9 0.3 collective-permute-start.1
  47.2 0.0 copy-start
  47.2 24.2 %attend.3 = (bf16[128,1024,128]{2,1,0:T(8,128)(2,1)}, bf16[128,1024,128]{2,1,0:T(8,128)(2,1)}, f32[17,64,128]{2,1,0:T(8,128)S(1)}, f32[17,64,128]{2,1,0:T(8,128)S(1)}) custom-call(s32[128]{0:T(128)S(1)} %copy-done.2, f32[2,128,16,128]{3,2,1,0:T(8,128)S(1)} %get-tuple-element.13.q_hbm, ...), custom_call_target="tpu_custom_call", output_to_operand_aliasing={{0}: (5, {}), {1}: (6, {})} | custom-call | flops 26843545600 | bytes 67108864 | tf_op jit(solution)/shard_map/attend/pallas_call | solution.py:158
  71.4 0.5 collective-permute-done.1.x_a
  71.9 0.0 collective-permute-done.2.diag_a
  71.9 0.0 collective-permute-done.core_a
  71.9 0.0 copy-done
  71.9 41.6 %combine.1 = bf16[128,8192]{1,0:T(8,128)(2,1)S(1)} custom-call(f32[17,64,128]{2,1,0:T(8,128)S(1)} %get-tuple-element.15.own_a, f32[17,64,128]{2,1,0:T(8,128)S(1)} %collective-permute-done.core_a, f32[17,64,128]{2,1,0:T(8,128)S(1)} %collective-permute-done.1.x_a, f32[17,64,128]{2,1,0:T(8,128)S(1)} %collective-permute-done.2.diag_a, ...), custom_call_target="tpu_custom_call" | custom-call | tf_op jit(solution)/shard_map/combine/pallas_call | solution.py:374
  113.5 1.3 %copy.18 = bf16[128,8192]{1,0:T(8,128)(2,1)} copy(bf16[128,8192]{1,0:T(8,128)(2,1)S(1)} %combine.1) | data formatting | bytes 4194304
Async XLA Ops:
  0.6 0.7 copy-start.1
  1.4 0.7 copy-start.2
  2.0 0.7 copy-start.3
  44.2 27.7 %collective-permute-start.2 = (f32[17,64,128]{2,1,0:T(8,128)S(1)}, f32[17,64,128]{2,1,0:T(8,128)S(1)}, u32[]{:S(2)}, u32[]{:S(2)}) collective-permute-start(f32[17,64,128]{2,1,0:T(8,128)S(1)} %get-tuple-element.16), channel_id=1, source_target_pairs={{0,3},{1,2},{2,1},{3,0},{4,7},{5,6},{6,5},{7,4}} | collective-permute-start | bytes 1671176 | tf_op jit(solution)/shard_map/ppermute | solution.py:558
  46.8 25.1 %collective-permute-start = (f32[17,64,128]{2,1,0:T(8,128)S(1)}, f32[17,64,128]{2,1,0:T(8,128)S(1)}, u32[]{:S(2)}, u32[]{:S(2)}) collective-permute-start(f32[17,64,128]{2,1,0:T(8,128)S(1)} %get-tuple-element.16), channel_id=1, source_target_pairs={{0,1},{1,0},{2,3},{3,2},{4,5},{5,4},{6,7},{7,6}} | collective-permute-start | bytes 1671176 | tf_op jit(solution)/shard_map/ppermute | solution.py:558
  46.9 25.0 %collective-permute-start.1 = (f32[17,64,128]{2,1,0:T(8,128)S(1)}, f32[17,64,128]{2,1,0:T(8,128)S(1)}, u32[]{:S(2)}, u32[]{:S(2)}) collective-permute-start(f32[17,64,128]{2,1,0:T(8,128)S(1)} %get-tuple-element.15.own_a), channel_id=1, source_target_pairs={{0,2},{1,3},{2,0},{3,1},{4,6},{5,7},{6,4},{7,5}} | collective-permute-start | bytes 1671176 | tf_op jit(solution)/shard_map/ppermute | solution.py:558
  47.2 24.7 %copy-start = (bf16[128,8192]{1,0:T(8,128)(2,1)S(1)}, bf16[128,8192]{1,0:T(8,128)(2,1)}, u32[]{:S(2)}) copy-start(bf16[128,8192]{1,0:T(8,128)(2,1)} %hid_hbm.3) | copy-start | bytes 6291460

commit v4 on v3

--- a/solution.py
+++ b/solution.py
@@ -181,8 +181,8 @@
 
 FIRST = 64
 PIECES = (64, 48, 16)
-MODES = 'QPD'
-LAGS = (0, 1, 0, 2, 3, 4)
+UNITS = ((0, 32, 'Q'), (0, 32, 'Q'), (1, 24, 'P'), (1, 24, 'P'), (2, 16, 'D'))
+ORDER = 'm0 s0 s1 h1 m1 h2 f0 f1 s2 m2 s3 f2 s4 f3 f4 l0 l1 l2 l3 l4 e0 e1 e2 e3 e4'
 MESH = pl.DeviceIdType.MESH
 
 
@@ -203,6 +203,9 @@
     first = own_a.shape[1]
     pieces = [(sum(PIECES[:j]), n) for j, n in enumerate(PIECES)]
     count = len(pieces)
+    units = [(sum(n for _, n, _ in UNITS[:u]), n) for u, (_, n, _) in enumerate(UNITS)]
+    units_of = [[u for u, unit in enumerate(UNITS) if unit[0] == j] for j in range(count)]
+    direct = [UNITS[us[0]][2] == 'D' for us in units_of]
     sp, y = lax.axis_index('sp'), lax.axis_index('tp')
     c, x = lax.rem(sp, 2), sp // 2
     to_c, to_x, to_y = {'sp': sp + 1 - 2 * c}, {'sp': sp + 2 - 4 * x}, {'tp': 1 - y}
@@ -213,10 +216,13 @@
     for dev in (to_c, to_x, to_y):
         pl.semaphore_signal(barrier, inc=1, device_id=dev, device_id_type=MESH)
 
-    w_copies = [pltpu.make_async_copy(w_hbm.at[:, pl.ds(pl.multiple_of((2 * sp + h) * cols, cols), cols)], w.at[h], w_sem.at[h]) for h in range(2)]
-    w_copies += [pltpu.make_async_copy(hid_hbm.at[:, pl.ds(pl.multiple_of((2 * sp + h) * cols, cols), cols)], hid.at[h], w_sem.at[2 + h]) for h in range(2)]
-    for cp in w_copies:
-        cp.start()
+    def w_copy(h):
+        return pltpu.make_async_copy(w_hbm.at[:, pl.ds(pl.multiple_of((2 * sp + h) * cols, cols), cols)], w.at[h], w_sem.at[h])
+
+    def hid_copy(h):
+        return pltpu.make_async_copy(hid_hbm.at[:, pl.ds(pl.multiple_of((2 * sp + h) * cols, cols), cols)], hid.at[h], w_sem.at[2 + h])
+
+    w_copy(1 - y).start()
     pl.semaphore_wait(barrier, 3)
 
     def copy(kind, j, src, dst, dev):
@@ -243,7 +249,7 @@
 
     own_att = att.at[pl.ds(c * half, half)]
     att_copies = [copy(4, j, own_att.at[:, at(j)], own_att.at[:, at(j)], to_c) for j in range(count)]
-    part_copies = [copy(5, j, part.at[1 - y, at(j)], r3.at[1 - y, at(j)], to_y) for j in range(count)]
+    part_copies = [copy(5, u, part.at[1 - y, pl.ds(*unit)], r3.at[1 - y, pl.ds(*unit)], to_y) for u, unit in enumerate(units)]
 
     parts_a = (own_a, core_a, x_a, diag_a)
     _, total, scales = weigh([p[half] for p in parts_a])
@@ -264,9 +270,13 @@
         for h in range(half):
             c1[h, local(j)] = own_b[h, local(j)] * scales[0][lo:lo + n, h:h + 1] + r1[h, local(j)] * scales[1][lo:lo + n, h:h + 1]
         push(x_copies[j])
-
-    def spread(kind, j, blk, dev):
-        return copy(kind, j, yall.at[blk, at(j)], yall.at[blk, at(j)], dev)
+    w_copy(y).start()
+    for h in range(2):
+        hid_copy(h).start()
+
+    def spread(kind, u, blk, dev):
+        rows = pl.ds(*units[u])
+        return copy(kind, u, yall.at[blk, rows], yall.at[blk, rows], dev)
 
     b_x, b_y, b_xy = block(1 - x, c, y), block(x, c, 1 - y), block(1 - x, c, 1 - y)
     final = {}
@@ -285,9 +295,6 @@
         push(att_copies[j])
 
     def multiply(j):
-        if j == 0:
-            for cp in w_copies:
-                cp.wait()
         att_copies[j].wait_recv()
         n = pieces[j][1]
         for h in range(heads):
@@ -300,64 +307,74 @@
                 return carry
             lax.fori_loop(0, cols // 256, tile, 0)
 
+        if j == 0:
+            w_copy(1 - y).wait()
         tiles(1 - y)
-        push(part_copies[j])
+        for u in units_of[j]:
+            push(part_copies[u])
+        if j == 0:
+            w_copy(y).wait()
         tiles(y)
-        if MODES[j] == 'D':
-            push(both_copy(j))
-
-    def both_copy(j):
-        return copy(13, j, part.at[y, at(j)], r3.at[y, at(j)], to_y)
-
-    def finish_sum(j):
-        part_copies[j].wait_recv()
-        if MODES[j] == 'D':
-            both_copy(j).wait_recv()
+        if direct[j]:
+            for u in units_of[j]:
+                push(both_copy(u))
+
+    def both_copy(u):
+        return copy(13, u, part.at[y, pl.ds(*units[u])], r3.at[y, pl.ds(*units[u])], to_y)
+
+    def finish_sum(u):
+        if u == 0:
+            for h in range(2):
+                hid_copy(h).wait()
+        rows = pl.ds(*units[u])
+        part_copies[u].wait_recv()
+        if UNITS[u][2] == 'D':
+            both_copy(u).wait_recv()
             for side in range(2):
-                yall[block(x, c, side), at(j)] = hid[side, at(j)].astype(jnp.float32) + (part[side, at(j)] + r3[side, at(j)])
-            push(spread(7, j, mine, to_x))
-            push(spread(10, j, b_y, to_x))
-            push(spread(6, j, mine, to_c))
-            push(spread(11, j, b_y, to_c))
+                yall[block(x, c, side), rows] = hid[side, rows].astype(jnp.float32) + (part[side, rows] + r3[side, rows])
+            push(spread(7, u, mine, to_x))
+            push(spread(10, u, b_y, to_x))
+            push(spread(6, u, mine, to_c))
+            push(spread(11, u, b_y, to_c))
             return
-        yall[mine, at(j)] = hid[y, at(j)].astype(jnp.float32) + (part[y, at(j)] + r3[y, at(j)])
-        push(spread(8, j, mine, to_y))
-        push(spread(7, j, mine, to_x))
-        push(spread(6, j, mine, to_c))
-
-    def forward(j):
+        yall[mine, rows] = hid[y, rows].astype(jnp.float32) + (part[y, rows] + r3[y, rows])
+        push(spread(8, u, mine, to_y))
+        push(spread(7, u, mine, to_x))
+        push(spread(6, u, mine, to_c))
+
+    def forward(u):
+        mode = UNITS[u][2]
+
         def from_x():
-            spread(7, j, b_x, to_x).wait_recv()
-            if MODES[j] == 'P':
-                push(spread(10, j, b_x, to_y))
-            push(spread(9, j, b_x, to_c))
+            spread(7, u, b_x, to_x).wait_recv()
+            if mode == 'P':
+                push(spread(10, u, b_x, to_y))
+            push(spread(9, u, b_x, to_c))
 
         def from_y():
-            spread(8, j, b_y, to_y).wait_recv()
-            if MODES[j] == 'Q':
-                push(spread(10, j, b_y, to_x))
-            push(spread(11, j, b_y, to_c))
-
-        for take in {'P': (from_x, from_y), 'Q': (from_y, from_x), 'D': (from_x,)}[MODES[j]]:
+            spread(8, u, b_y, to_y).wait_recv()
+            if mode == 'Q':
+                push(spread(10, u, b_y, to_x))
+            push(spread(11, u, b_y, to_c))
+
+        for take in {'P': (from_x, from_y), 'Q': (from_y, from_x), 'D': (from_x,)}[mode]:
             take()
 
-    def forward_last(j):
-        spread(10, j, b_xy, to_y).wait_recv()
-        push(spread(12, j, b_xy, to_c))
-
-    def emit(j):
-        spread(6, j, block(x, 1 - c, y), to_c).wait_recv()
-        spread(9, j, block(1 - x, 1 - c, y), to_c).wait_recv()
-        spread(11, j, block(x, 1 - c, 1 - y), to_c).wait_recv()
-        spread(12, j, block(1 - x, 1 - c, 1 - y), to_c).wait_recv()
+    def forward_last(u):
+        spread(10, u, b_xy, to_y).wait_recv()
+        push(spread(12, u, b_xy, to_c))
+
+    def emit(u):
+        spread(6, u, block(x, 1 - c, y), to_c).wait_recv()
+        spread(9, u, block(1 - x, 1 - c, y), to_c).wait_recv()
+        spread(11, u, block(x, 1 - c, 1 - y), to_c).wait_recv()
+        spread(12, u, block(1 - x, 1 - c, 1 - y), to_c).wait_recv()
         for g in range(8):
-            y_ref[at(j), g * cols:(g + 1) * cols] = yall[g, at(j)].astype(y_ref.dtype)
-
-    stages = tuple(zip((finish_heads, finish_sum, multiply, forward, forward_last, emit), LAGS))
-    for t in range(count + max(LAGS)):
-        for stage, lag in stages:
-            if 0 <= t - lag < count:
-                stage(t - lag)
+            y_ref[pl.ds(*units[u]), g * cols:(g + 1) * cols] = yall[g, pl.ds(*units[u])].astype(y_ref.dtype)
+
+    stages = {'h': finish_heads, 's': finish_sum, 'm': multiply, 'f': forward, 'l': forward_last, 'e': emit}
+    for name in ORDER.split():
+        stages[name[0]](int(name[1:]))
     for cp in pending:
         cp.wait_send()
 
@@ -370,7 +387,7 @@
     heads = 2 * half
     cols = w_o.shape[1] // 8
     f32 = jnp.float32
-    kinds, count = 14, len(PIECES)
+    kinds, count = 14, max(len(PIECES), len(UNITS))
     return pl.pallas_call(
         combine_kernel,
         out_shape=jax.ShapeDtypeStruct(hidden.shape, hidden.dtype),

time: 115 us -> 112 us (0.974)
  Pallas kernels: 107 us -> 104 us
    pallas_call x1, Pallas kernels: 41.6 us -> 38.8 us  [combine_and_project(): pl.pallas_call(combine_kernel, out_shape=jax.ShapeDtypeStruct(hidden.shap...]
  transfers between devices with their start and end apart: 3 -> 3, of which waited for: 1 -> 1; matrix products, arithmetic and copies ran while one was open for 0% -> 0% of each run, Pallas kernels for 21% -> 22%
where the time goes in v4:
time: 112 us
  Pallas kernels  104 us (93%)
  local copies, waits for them, and re-layouts  3.35 us (3%)
  starting transfers between devices  3.04 us (3%)
    pallas_call x2, Pallas kernels, write_and_attend(): pl.pallas_call(functools.partial(attend_kernel, first, count), out_shape=...  48.4 us
    pallas_call x1, Pallas kernels, combine_and_project(): pl.pallas_call(combine_kernel, out_shape=jax.ShapeDtypeStruct(hidden.shap...  38.8 us
    pallas_call x1, Pallas kernels, project(): pl.pallas_call(project_kernel, out_shape=(jax.ShapeDtypeStruct((2, batch,...  17.3 us
    unnamed x9, local copies, waits for them, and re-layouts  3.35 us
    ppermute x3, starting transfers between devices, device_step(): lax.ppermute(array, 'sp', [(s, s ^ flip) for s in range(4)])  3.04 us
  transfers between devices with their start and end apart: 3, of which 1 were waited for; matrix products, arithmetic and copies ran while one was open for 0% of the time, Pallas kernels for 22%

profile of v4, /device:TPU:0, one launch (start us, length us, event | category | flops | bytes accessed | tf_op | source)
XLA Modules:
  0.0 112.0 jit_solution(3806196248209915424)
XLA Ops:
  0.6 0.0 copy-start.1
  0.6 0.7 copy-done.1
  1.4 0.0 copy-start.2
  1.4 0.7 copy-done.2
  2.0 0.0 copy-start.3
  2.0 0.7 copy-done.3
  2.7 17.3 %project.1 = (f32[2,128,16,128]{3,2,1,0:T(8,128)S(1)}, f32[2,128,4,128]{3,2,1,0:T(4,128)S(1)}) custom-call(bf16[128,8192]{1,0:T(8,128)(2,1)} %hid_hbm.3, bf16[64,128]{1,0:T(8,128)(2,1)S(1)} %bitcast.7, s32[1,128]{1,0:T(1,128)S(1)} %bitcast.8, f32[1,64]{1,0:T(1,128)S(1)} %bitcast.9, bf16[8192,4096]{1,0:T(8,128)(2,1)} %wq_hbm.1, bf16[8192,512]{1,0:T(8,128)(2,1)} %wk_hbm.1, ...), custom_call_target="tpu_custom_call" | custom-call | tf_op jit(solution)/shard_map/project/pallas_call | solution.py:541
  20.0 24.2 %attend.2 = (bf16[128,1024,128]{2,1,0:T(8,128)(2,1)}, bf16[128,1024,128]{2,1,0:T(8,128)(2,1)}, f32[17,64,128]{2,1,0:T(8,128)S(1)}, f32[17,64,128]{2,1,0:T(8,128)S(1)}) custom-call(s32[128]{0:T(128)S(1)} %copy-done.2, f32[2,128,16,128]{3,2,1,0:T(8,128)S(1)} %get-tuple-element.13.q_hbm, f32[2,128,4,128]{3,2,1,0:T(4,128)S(1)} %get-tuple-element.14.kv_hbm, ...), custom_call_target="tpu_custom_call" | custom-call | flops 26843545600 | bytes 67108864 | tf_op jit(solution)/shard_map/attend/pallas_call | solution.py:158
  44.2 2.6 %collective-permute-start.2 = (f32[17,64,128]{2,1,0:T(8,128)S(1)}, f32[17,64,128]{2,1,0:T(8,128)S(1)}, u32[]{:S(2)}, u32[]{:S(2)}) collective-permute-start(f32[17,64,128]{2,1,0:T(8,128)S(1)} %get-tuple-element.16), channel_id=1, source_target_pairs={{0,3},{1,2},{2,1},{3,0},{4,7},{5,6},{6,5},{7,4}} | collective-permute-start | bytes 1671176 | tf_op jit(solution)/shard_map/ppermute | solution.py:575
  46.8 0.1 collective-permute-start
  46.9 0.3 collective-permute-start.1
  47.2 0.0 copy-start
  47.2 24.2 %attend.3 = (bf16[128,1024,128]{2,1,0:T(8,128)(2,1)}, bf16[128,1024,128]{2,1,0:T(8,128)(2,1)}, f32[17,64,128]{2,1,0:T(8,128)S(1)}, f32[17,64,128]{2,1,0:T(8,128)S(1)}) custom-call(s32[128]{0:T(128)S(1)} %copy-done.2, f32[2,128,16,128]{3,2,1,0:T(8,128)S(1)} %get-tuple-element.13.q_hbm, ...), custom_call_target="tpu_custom_call", output_to_operand_aliasing={{0}: (5, {}), {1}: (6, {})} | custom-call | flops 26843545600 | bytes 67108864 | tf_op jit(solution)/shard_map/attend/pallas_call | solution.py:158
  71.4 0.5 collective-permute-done.1.x_a
  71.9 0.0 collective-permute-done.2.diag_a
  71.9 0.0 collective-permute-done.core_a
  71.9 0.0 copy-done
  71.9 38.8 %combine.1 = bf16[128,8192]{1,0:T(8,128)(2,1)S(1)} custom-call(f32[17,64,128]{2,1,0:T(8,128)S(1)} %get-tuple-element.15.own_a, f32[17,64,128]{2,1,0:T(8,128)S(1)} %collective-permute-done.core_a, f32[17,64,128]{2,1,0:T(8,128)S(1)} %collective-permute-done.1.x_a, f32[17,64,128]{2,1,0:T(8,128)S(1)} %collective-permute-done.2.diag_a, ...), custom_call_target="tpu_custom_call" | custom-call | tf_op jit(solution)/shard_map/combine/pallas_call | solution.py:391
  110.7 1.3 %copy.18 = bf16[128,8192]{1,0:T(8,128)(2,1)} copy(bf16[128,8192]{1,0:T(8,128)(2,1)S(1)} %combine.1) | data formatting | bytes 4194304
Async XLA Ops:
  0.6 0.7 copy-start.1
  1.4 0.7 copy-start.2
  2.0 0.7 copy-start.3
  44.2 27.7 %collective-permute-start.2 = (f32[17,64,128]{2,1,0:T(8,128)S(1)}, f32[17,64,128]{2,1,0:T(8,128)S(1)}, u32[]{:S(2)}, u32[]{:S(2)}) collective-permute-start(f32[17,64,128]{2,1,0:T(8,128)S(1)} %get-tuple-element.16), channel_id=1, source_target_pairs={{0,3},{1,2},{2,1},{3,0},{4,7},{5,6},{6,5},{7,4}} | collective-permute-start | bytes 1671176 | tf_op jit(solution)/shard_map/ppermute | solution.py:575
  46.8 25.1 %collective-permute-start = (f32[17,64,128]{2,1,0:T(8,128)S(1)}, f32[17,64,128]{2,1,0:T(8,128)S(1)}, u32[]{:S(2)}, u32[]{:S(2)}) collective-permute-start(f32[17,64,128]{2,1,0:T(8,128)S(1)} %get-tuple-element.16), channel_id=1, source_target_pairs={{0,1},{1,0},{2,3},{3,2},{4,5},{5,4},{6,7},{7,6}} | collective-permute-start | bytes 1671176 | tf_op jit(solution)/shard_map/ppermute | solution.py:575
  46.9 25.0 %collective-permute-start.1 = (f32[17,64,128]{2,1,0:T(8,128)S(1)}, f32[17,64,128]{2,1,0:T(8,128)S(1)}, u32[]{:S(2)}, u32[]{:S(2)}) collective-permute-start(f32[17,64,128]{2,1,0:T(8,128)S(1)} %get-tuple-element.15.own_a), channel_id=1, source_target_pairs={{0,2},{1,3},{2,0},{3,1},{4,6},{5,7},{6,4},{7,5}} | collective-permute-start | bytes 1671176 | tf_op jit(solution)/shard_map/ppermute | solution.py:575
  47.2 24.7 %copy-start = (bf16[128,8192]{1,0:T(8,128)(2,1)S(1)}, bf16[128,8192]{1,0:T(8,128)(2,1)}, u32[]{:S(2)}) copy-start(bf16[128,8192]{1,0:T(8,128)(2,1)} %hid_hbm.3) | copy-start | bytes 6291460

commit v5 on v4

--- a/solution.py
+++ b/solution.py
@@ -182,7 +182,8 @@
 FIRST = 64
 PIECES = (64, 48, 16)
 UNITS = ((0, 32, 'Q'), (0, 32, 'Q'), (1, 24, 'P'), (1, 24, 'P'), (2, 16, 'D'))
-ORDER = 'm0 s0 s1 h1 m1 h2 f0 f1 s2 m2 s3 f2 s4 f3 f4 l0 l1 l2 l3 l4 e0 e1 e2 e3 e4'
+ORDER = ('m0', 's0', 's1', 'h1', 'm1', 'h2', 'f0', 'f1', 's2', 'm2', 's3', 'f2', 's4',
+         'f3', 'f4', 'l0', 'l1', 'l2', 'l3', 'l4', 'e0', 'e1', 'e2', 'e3', 'e4')
 MESH = pl.DeviceIdType.MESH
 
 
@@ -373,7 +374,7 @@
             y_ref[pl.ds(*units[u]), g * cols:(g + 1) * cols] = yall[g, pl.ds(*units[u])].astype(y_ref.dtype)
 
     stages = {'h': finish_heads, 's': finish_sum, 'm': multiply, 'f': forward, 'l': forward_last, 'e': emit}
-    for name in ORDER.split():
+    for name in ORDER:
         stages[name[0]](int(name[1:]))
     for cp in pending:
         cp.wait_send()

time: 112 us -> 112 us (level)
  no operation moved by 1% of the time
where the time goes in v5:
time: 112 us
  Pallas kernels  104 us (93%)
  local copies, waits for them, and re-layouts  3.35 us (3%)
  starting transfers between devices  3.04 us (3%)
    pallas_call x2, Pallas kernels, write_and_attend(): pl.pallas_call(functools.partial(attend_kernel, first, count), out_shape=...  48.4 us
    pallas_call x1, Pallas kernels, combine_and_project(): pl.pallas_call(combine_kernel, out_shape=jax.ShapeDtypeStruct(hidden.shap...  38.8 us
    pallas_call x1, Pallas kernels, project(): pl.pallas_call(project_kernel, out_shape=(jax.ShapeDtypeStruct((2, batch,...  17.3 us
    unnamed x9, local copies, waits for them, and re-layouts  3.35 us
    ppermute x3, starting transfers between devices, device_step(): lax.ppermute(array, 'sp', [(s, s ^ flip) for s in range(4)])  3.04 us
  transfers between devices with their start and end apart: 3, of which 1 were waited for; matrix products, arithmetic and copies ran while one was open for 0% of the time, Pallas kernels for 22%

profile of v5, /device:TPU:0, one launch (start us, length us, event | category | flops | bytes accessed | tf_op | source)
XLA Modules:
  0.0 112.0 jit_solution(3806196248209915424)
XLA Ops:
  0.6 0.0 copy-start.1
  0.6 0.7 copy-done.1
  1.4 0.0 copy-start.2
  1.4 0.7 copy-done.2
  2.0 0.0 copy-start.3
  2.0 0.7 copy-done.3
  2.7 17.3 %project.1 = (f32[2,128,16,128]{3,2,1,0:T(8,128)S(1)}, f32[2,128,4,128]{3,2,1,0:T(4,128)S(1)}) custom-call(bf16[128,8192]{1,0:T(8,128)(2,1)} %hid_hbm.3, bf16[64,128]{1,0:T(8,128)(2,1)S(1)} %bitcast.7, s32[1,128]{1,0:T(1,128)S(1)} %bitcast.8, f32[1,64]{1,0:T(1,128)S(1)} %bitcast.9, bf16[8192,4096]{1,0:T(8,128)(2,1)} %wq_hbm.1, bf16[8192,512]{1,0:T(8,128)(2,1)} %wk_hbm.1, ...), custom_call_target="tpu_custom_call" | custom-call | tf_op jit(solution)/shard_map/project/pallas_call | solution.py:542
  20.0 24.2 %attend.2 = (bf16[128,1024,128]{2,1,0:T(8,128)(2,1)}, bf16[128,1024,128]{2,1,0:T(8,128)(2,1)}, f32[17,64,128]{2,1,0:T(8,128)S(1)}, f32[17,64,128]{2,1,0:T(8,128)S(1)}) custom-call(s32[128]{0:T(128)S(1)} %copy-done.2, f32[2,128,16,128]{3,2,1,0:T(8,128)S(1)} %get-tuple-element.13.q_hbm, f32[2,128,4,128]{3,2,1,0:T(4,128)S(1)} %get-tuple-element.14.kv_hbm, ...), custom_call_target="tpu_custom_call" | custom-call | flops 26843545600 | bytes 67108864 | tf_op jit(solution)/shard_map/attend/pallas_call | solution.py:158
  44.2 2.6 %collective-permute-start.2 = (f32[17,64,128]{2,1,0:T(8,128)S(1)}, f32[17,64,128]{2,1,0:T(8,128)S(1)}, u32[]{:S(2)}, u32[]{:S(2)}) collective-permute-start(f32[17,64,128]{2,1,0:T(8,128)S(1)} %get-tuple-element.16), channel_id=1, source_target_pairs={{0,3},{1,2},{2,1},{3,0},{4,7},{5,6},{6,5},{7,4}} | collective-permute-start | bytes 1671176 | tf_op jit(solution)/shard_map/ppermute | solution.py:576
  46.8 0.1 collective-permute-start
  46.9 0.3 collective-permute-start.1
  47.2 0.0 copy-start
  47.2 24.2 %attend.3 = (bf16[128,1024,128]{2,1,0:T(8,128)(2,1)}, bf16[128,1024,128]{2,1,0:T(8,128)(2,1)}, f32[17,64,128]{2,1,0:T(8,128)S(1)}, f32[17,64,128]{2,1,0:T(8,128)S(1)}) custom-call(s32[128]{0:T(128)S(1)} %copy-done.2, f32[2,128,16,128]{3,2,1,0:T(8,128)S(1)} %get-tuple-element.13.q_hbm, ...), custom_call_target="tpu_custom_call", output_to_operand_aliasing={{0}: (5, {}), {1}: (6, {})} | custom-call | flops 26843545600 | bytes 67108864 | tf_op jit(solution)/shard_map/attend/pallas_call | solution.py:158
  71.4 0.5 collective-permute-done.1.x_a
  71.9 0.0 collective-permute-done.2.diag_a
  71.9 0.0 collective-permute-done.core_a
  71.9 0.0 copy-done
  71.9 38.8 %combine.1 = bf16[128,8192]{1,0:T(8,128)(2,1)S(1)} custom-call(f32[17,64,128]{2,1,0:T(8,128)S(1)} %get-tuple-element.15.own_a, f32[17,64,128]{2,1,0:T(8,128)S(1)} %collective-permute-done.core_a, f32[17,64,128]{2,1,0:T(8,128)S(1)} %collective-permute-done.1.x_a, f32[17,64,128]{2,1,0:T(8,128)S(1)} %collective-permute-done.2.diag_a, ...), custom_call_target="tpu_custom_call" | custom-call | tf_op jit(solution)/shard_map/combine/pallas_call | solution.py:392
  110.7 1.3 %copy.18 = bf16[128,8192]{1,0:T(8,128)(2,1)} copy(bf16[128,8192]{1,0:T(8,128)(2,1)S(1)} %combine.1) | data formatting | bytes 4194304
Async XLA Ops:
  0.6 0.7 copy-start.1
  1.4 0.7 copy-start.2
  2.0 0.7 copy-start.3
  44.2 27.7 %collective-permute-start.2 = (f32[17,64,128]{2,1,0:T(8,128)S(1)}, f32[17,64,128]{2,1,0:T(8,128)S(1)}, u32[]{:S(2)}, u32[]{:S(2)}) collective-permute-start(f32[17,64,128]{2,1,0:T(8,128)S(1)} %get-tuple-element.16), channel_id=1, source_target_pairs={{0,3},{1,2},{2,1},{3,0},{4,7},{5,6},{6,5},{7,4}} | collective-permute-start | bytes 1671176 | tf_op jit(solution)/shard_map/ppermute | solution.py:576
  46.8 25.1 %collective-permute-start = (f32[17,64,128]{2,1,0:T(8,128)S(1)}, f32[17,64,128]{2,1,0:T(8,128)S(1)}, u32[]{:S(2)}, u32[]{:S(2)}) collective-permute-start(f32[17,64,128]{2,1,0:T(8,128)S(1)} %get-tuple-element.16), channel_id=1, source_target_pairs={{0,1},{1,0},{2,3},{3,2},{4,5},{5,4},{6,7},{7,6}} | collective-permute-start | bytes 1671176 | tf_op jit(solution)/shard_map/ppermute | solution.py:576
  46.9 25.0 %collective-permute-start.1 = (f32[17,64,128]{2,1,0:T(8,128)S(1)}, f32[17,64,128]{2,1,0:T(8,128)S(1)}, u32[]{:S(2)}, u32[]{:S(2)}) collective-permute-start(f32[17,64,128]{2,1,0:T(8,128)S(1)} %get-tuple-element.15.own_a), channel_id=1, source_target_pairs={{0,2},{1,3},{2,0},{3,1},{4,6},{5,7},{6,4},{7,5}} | collective-permute-start | bytes 1671176 | tf_op jit(solution)/shard_map/ppermute | solution.py:576
  47.2 24.7 %copy-start = (bf16[128,8192]{1,0:T(8,128)(2,1)S(1)}, bf16[128,8192]{1,0:T(8,128)(2,1)}, u32[]{:S(2)}) copy-start(bf16[128,8192]{1,0:T(8,128)(2,1)} %hid_hbm.3) | copy-start | bytes 6291460

commit v6 on v5

--- a/solution.py
+++ b/solution.py
@@ -183,7 +183,7 @@
 PIECES = (64, 48, 16)
 UNITS = ((0, 32, 'Q'), (0, 32, 'Q'), (1, 24, 'P'), (1, 24, 'P'), (2, 16, 'D'))
 ORDER = ('m0', 's0', 's1', 'h1', 'm1', 'h2', 'f0', 'f1', 's2', 'm2', 's3', 'f2', 's4',
-         'f3', 'f4', 'l0', 'l1', 'l2', 'l3', 'l4', 'e0', 'e1', 'e2', 'e3', 'e4')
+         'f3', 'f4', 'l0', 'l1', 'l4', 'l2', 'e0', 'e1', 'e4', 'e2', 'l3', 'e3')
 MESH = pl.DeviceIdType.MESH
 
 

time: 112 us -> 113 us (level)
  transfers between devices with their start and end apart: 3 -> 3, of which waited for: 1 -> 1; matrix products, arithmetic and copies ran while one was open for 0% -> 0% of each run, Pallas kernels for 22% -> 21%
where the time goes in v6:
time: 113 us
  Pallas kernels  105 us (93%)
  local copies, waits for them, and re-layouts  3.35 us (3%)
  starting transfers between devices  3.04 us (3%)
    pallas_call x2, Pallas kernels, write_and_attend(): pl.pallas_call(functools.partial(attend_kernel, first, count), out_shape=...  48.4 us
    pallas_call x1, Pallas kernels, combine_and_project(): pl.pallas_call(combine_kernel, out_shape=jax.ShapeDtypeStruct(hidden.shap...  39.3 us
    pallas_call x1, Pallas kernels, project(): pl.pallas_call(project_kernel, out_shape=(jax.ShapeDtypeStruct((2, batch,...  17.3 us
    unnamed x9, local copies, waits for them, and re-layouts  3.35 us
    ppermute x3, starting transfers between devices, device_step(): lax.ppermute(array, 'sp', [(s, s ^ flip) for s in range(4)])  3.04 us
  transfers between devices with their start and end apart: 3, of which 1 were waited for; matrix products, arithmetic and copies ran while one was open for 0% of the time, Pallas kernels for 21%

profile of v6, /device:TPU:0, one launch (start us, length us, event | category | flops | bytes accessed | tf_op | source)
XLA Modules:
  0.0 112.5 jit_solution(18316633038740391713)
XLA Ops:
  0.6 0.0 copy-start.1
  0.6 0.7 copy-done.1
  1.4 0.0 copy-start.2
  1.4 0.7 copy-done.2
  2.0 0.0 copy-start.3
  2.0 0.7 copy-done.3
  2.7 17.3 %project.1 = (f32[2,128,16,128]{3,2,1,0:T(8,128)S(1)}, f32[2,128,4,128]{3,2,1,0:T(4,128)S(1)}) custom-call(bf16[128,8192]{1,0:T(8,128)(2,1)} %hid_hbm.3, bf16[64,128]{1,0:T(8,128)(2,1)S(1)} %bitcast.7, s32[1,128]{1,0:T(1,128)S(1)} %bitcast.8, f32[1,64]{1,0:T(1,128)S(1)} %bitcast.9, bf16[8192,4096]{1,0:T(8,128)(2,1)} %wq_hbm.1, bf16[8192,512]{1,0:T(8,128)(2,1)} %wk_hbm.1, ...), custom_call_target="tpu_custom_call" | custom-call | tf_op jit(solution)/shard_map/project/pallas_call | solution.py:542
  20.0 24.2 %attend.2 = (bf16[128,1024,128]{2,1,0:T(8,128)(2,1)}, bf16[128,1024,128]{2,1,0:T(8,128)(2,1)}, f32[17,64,128]{2,1,0:T(8,128)S(1)}, f32[17,64,128]{2,1,0:T(8,128)S(1)}) custom-call(s32[128]{0:T(128)S(1)} %copy-done.2, f32[2,128,16,128]{3,2,1,0:T(8,128)S(1)} %get-tuple-element.13.q_hbm, f32[2,128,4,128]{3,2,1,0:T(4,128)S(1)} %get-tuple-element.14.kv_hbm, ...), custom_call_target="tpu_custom_call" | custom-call | flops 26843545600 | bytes 67108864 | tf_op jit(solution)/shard_map/attend/pallas_call | solution.py:158
  44.2 2.6 %collective-permute-start.2 = (f32[17,64,128]{2,1,0:T(8,128)S(1)}, f32[17,64,128]{2,1,0:T(8,128)S(1)}, u32[]{:S(2)}, u32[]{:S(2)}) collective-permute-start(f32[17,64,128]{2,1,0:T(8,128)S(1)} %get-tuple-element.16), channel_id=1, source_target_pairs={{0,3},{1,2},{2,1},{3,0},{4,7},{5,6},{6,5},{7,4}} | collective-permute-start | bytes 1671176 | tf_op jit(solution)/shard_map/ppermute | solution.py:576
  46.8 0.1 collective-permute-start
  46.9 0.3 collective-permute-start.1
  47.2 0.0 copy-start
  47.2 24.2 %attend.3 = (bf16[128,1024,128]{2,1,0:T(8,128)(2,1)}, bf16[128,1024,128]{2,1,0:T(8,128)(2,1)}, f32[17,64,128]{2,1,0:T(8,128)S(1)}, f32[17,64,128]{2,1,0:T(8,128)S(1)}) custom-call(s32[128]{0:T(128)S(1)} %copy-done.2, f32[2,128,16,128]{3,2,1,0:T(8,128)S(1)} %get-tuple-element.13.q_hbm, ...), custom_call_target="tpu_custom_call", output_to_operand_aliasing={{0}: (5, {}), {1}: (6, {})} | custom-call | flops 26843545600 | bytes 67108864 | tf_op jit(solution)/shard_map/attend/pallas_call | solution.py:158
  71.4 0.5 collective-permute-done.1.x_a
  71.9 0.0 collective-permute-done.2.diag_a
  71.9 0.0 collective-permute-done.core_a
  71.9 0.0 copy-done
  71.9 39.3 %combine.1 = bf16[128,8192]{1,0:T(8,128)(2,1)S(1)} custom-call(f32[17,64,128]{2,1,0:T(8,128)S(1)} %get-tuple-element.15.own_a, f32[17,64,128]{2,1,0:T(8,128)S(1)} %collective-permute-done.core_a, f32[17,64,128]{2,1,0:T(8,128)S(1)} %collective-permute-done.1.x_a, f32[17,64,128]{2,1,0:T(8,128)S(1)} %collective-permute-done.2.diag_a, ...), custom_call_target="tpu_custom_call" | custom-call | tf_op jit(solution)/shard_map/combine/pallas_call | solution.py:392
  111.2 1.3 %copy.18 = bf16[128,8192]{1,0:T(8,128)(2,1)} copy(bf16[128,8192]{1,0:T(8,128)(2,1)S(1)} %combine.1) | data formatting | bytes 4194304
Async XLA Ops:
  0.6 0.7 copy-start.1
  1.4 0.7 copy-start.2
  2.0 0.7 copy-start.3
  44.2 27.7 %collective-permute-start.2 = (f32[17,64,128]{2,1,0:T(8,128)S(1)}, f32[17,64,128]{2,1,0:T(8,128)S(1)}, u32[]{:S(2)}, u32[]{:S(2)}) collective-permute-start(f32[17,64,128]{2,1,0:T(8,128)S(1)} %get-tuple-element.16), channel_id=1, source_target_pairs={{0,3},{1,2},{2,1},{3,0},{4,7},{5,6},{6,5},{7,4}} | collective-permute-start | bytes 1671176 | tf_op jit(solution)/shard_map/ppermute | solution.py:576
  46.8 25.1 %collective-permute-start = (f32[17,64,128]{2,1,0:T(8,128)S(1)}, f32[17,64,128]{2,1,0:T(8,128)S(1)}, u32[]{:S(2)}, u32[]{:S(2)}) collective-permute-start(f32[17,64,128]{2,1,0:T(8,128)S(1)} %get-tuple-element.16), channel_id=1, source_target_pairs={{0,1},{1,0},{2,3},{3,2},{4,5},{5,4},{6,7},{7,6}} | collective-permute-start | bytes 1671176 | tf_op jit(solution)/shard_map/ppermute | solution.py:576
  46.9 25.0 %collective-permute-start.1 = (f32[17,64,128]{2,1,0:T(8,128)S(1)}, f32[17,64,128]{2,1,0:T(8,128)S(1)}, u32[]{:S(2)}, u32[]{:S(2)}) collective-permute-start(f32[17,64,128]{2,1,0:T(8,128)S(1)} %get-tuple-element.15.own_a), channel_id=1, source_target_pairs={{0,2},{1,3},{2,0},{3,1},{4,6},{5,7},{6,4},{7,5}} | collective-permute-start | bytes 1671176 | tf_op jit(solution)/shard_map/ppermute | solution.py:576
  47.2 24.7 %copy-start = (bf16[128,8192]{1,0:T(8,128)(2,1)S(1)}, bf16[128,8192]{1,0:T(8,128)(2,1)}, u32[]{:S(2)}) copy-start(bf16[128,8192]{1,0:T(8,128)(2,1)} %hid_hbm.3) | copy-start | bytes 6291460
